TPU v7x, 1024 devices: a whole 8x8x8 slice. The times are simulated.
1024 devices in a mesh: replica: 16 (over z, core), fsdp: 64 (over x, y).
Axes of the slice: x: 8, y: 8, z: 8, core: 2. Of those that a mesh axis runs over, the one named last changes fastest.
Arguments:
- states: bfloat16 [1024, 256, 2048], P(('replica', 'fsdp'))
- cotangent: bfloat16 [1024, 256, 512], P(('replica', 'fsdp')), may hold values from -6 to 6
- kv_weight: bfloat16 [2048, 512], P('fsdp'), may hold values from -0.125 to 0.125
- norm_gain: bfloat16 [2048], P('fsdp'), may hold values from -1.5 to 1.5
- prompt_len: int32 [1024], P(('replica', 'fsdp')), may hold values from 1 to 255, as said below
- response_len: int32 [1024], P(('replica', 'fsdp')), may hold values from 1 to 192
- reward_bucket: int32 [1024], P(('replica', 'fsdp')), may hold values from 0 to 10, as said below
Outputs:
- key_values: bfloat16 [1024, 256, 512], P(('replica', 'fsdp'))
- grad_weight: float32 [2048, 512], P('fsdp')
- grad_gain: float32 [2048], P('fsdp')
Inputs may be any that keep to these rules, and one draw needn't show every extreme that they name: prompt_len + response_len <= 256 for every rollout. `reward_bucket`: some rollout has level 0 and some has level 10.
All inputs are finite; a program needn't handle non-finite values.
Results may differ from a plain program's by a relative error of at most 0.005.
Values may be sent and summed in bfloat16 or wider, within the bound.
No kernel may reach another device: no remote copies, remote signals or barrier semaphores. Data moves between devices by JAX's collectives and lax.ppermute only.
A program may use at most 64 MiB of HBM per device.

v0:
```python
import functools
import math

import jax
import jax.numpy as jnp
from jax import lax
from jax.sharding import Mesh
from jax.sharding import PartitionSpec as P

FSDP = ("fsdp_0", "fsdp_1")
REPLICA_FSDP = ("replica_0", "replica_1", "fsdp_0", "fsdp_1")
REPLICA = ("replica_0", "replica_1")


EPSILON = 1e-06
BLOCK_ROWS = 32


def side_by_side(arrays, axis, dim, along):
    widths = [math.prod(a.shape[along:]) for a in arrays]
    both = jnp.concatenate(
        [a.reshape(*a.shape[:along], w) for a, w in zip(arrays, widths)], axis=along
    )
    filled = lax.all_gather(both, axis, axis=dim, tiled=True)
    pieces = jnp.split(filled, [sum(widths[:k]) for k in range(1, len(widths))], axis=along)
    return tuple(
        (b.reshape(*filled.shape[:along], *a.shape[along:]) for a, b in zip(arrays, pieces))
    )


def over_axes(value, axes):
    return functools.reduce(lax.psum, axes, value)


def in_one_piece(arrays, axis, dim, along):
    widths = [math.prod(a.shape[along:]) for a in arrays]
    both = jnp.concatenate(
        [a.reshape(*a.shape[:along], w) for a, w in zip(arrays, widths)], axis=along
    )
    filled = lax.psum_scatter(both, axis, scatter_dimension=dim, tiled=True)
    pieces = jnp.split(filled, [sum(widths[:k]) for k in range(1, len(widths))], axis=along)
    return tuple(
        (b.reshape(*filled.shape[:along], *a.shape[along:]) for a, b in zip(arrays, pieces))
    )


def total_of_pieces(value, axis):
    pieces = lax.all_gather(value, axis)
    return pieces.sum(axis=0)


def normalize(states, gain_wide):
    widened = states.astype(jnp.float32)
    unit_rows = widened * lax.rsqrt(jnp.mean(widened * widened, axis=-1, keepdims=True) + EPSILON)
    return (unit_rows, (unit_rows * (1.0 + gain_wide)).astype(jnp.bfloat16))


def accumulate(unit_rows, normed, cotangent, coefficient, live_flag, weight_full):
    ordering = jnp.argsort(1 - live_flag, stable=True)
    unit_rows = jnp.take(unit_rows, ordering, axis=0)
    normed = jnp.take(normed, ordering, axis=0)
    cotangent = jnp.take(cotangent, ordering, axis=0)
    coefficient = jnp.take(coefficient, ordering, axis=0)
    row_total = normed.shape[0]
    width = normed.shape[1]
    feature_count = cotangent.shape[1]
    block_span = min(BLOCK_ROWS, row_total)
    block_count = (jnp.sum(live_flag) + block_span - 1) // block_span
    grad_shape = (width, feature_count)

    def one_block(step_index, totals):
        grad_weight, grad_gain = totals
        first_row = step_index * block_span
        unit_part = lax.dynamic_slice_in_dim(unit_rows, first_row, block_span, 0)
        normed_part = lax.dynamic_slice_in_dim(normed, first_row, block_span, 0)
        coef_part = lax.dynamic_slice_in_dim(coefficient, first_row, block_span, 0)
        cot_part = lax.dynamic_slice_in_dim(cotangent, first_row, block_span, 0)
        weighted = (coef_part[:, None] * cot_part.astype(jnp.float32)).astype(jnp.bfloat16)
        outer_part = jnp.einsum(
            "td,tk->dk", normed_part, weighted, preferred_element_type=jnp.float32
        )
        backward = jnp.einsum(
            "tk,dk->td", weighted, weight_full, preferred_element_type=jnp.float32
        )
        return (grad_weight + outer_part, grad_gain + jnp.sum(unit_part * backward, axis=0))

    start_totals = (jnp.zeros(grad_shape, jnp.float32), jnp.zeros((width,), jnp.float32))
    grad_weight, grad_gain = lax.fori_loop(0, block_count, one_block, start_totals)
    return (grad_weight, grad_gain)


def shards(states, cotangent, kv_weight, norm_gain, prompt_len, response_len, reward_bucket):
    weight_full, gain_full = side_by_side((kv_weight, norm_gain), FSDP, 0, 1)
    gain_wide = gain_full.astype(jnp.float32)
    seq_states = states[0]
    seq_cotangent = cotangent[0]
    row_total = seq_states.shape[0]
    unit_rows, normed = normalize(seq_states, gain_wide)
    key_values = jnp.dot(normed, weight_full, preferred_element_type=jnp.float32).astype(
        jnp.bfloat16
    )[None]
    position = jnp.arange(row_total, dtype=jnp.int32)
    live_flag = ((position >= prompt_len[0]) & (position < prompt_len[0] + response_len[0])).astype(
        jnp.int32
    )
    reward_value = reward_bucket.astype(jnp.float32)
    reward_sum, square_sum, token_total = (
        over_axes(reward_value, REPLICA_FSDP),
        over_axes(reward_value * reward_value, REPLICA_FSDP),
        over_axes(response_len.astype(jnp.float32), REPLICA_FSDP),
    )
    rollout_count = lax.axis_size(REPLICA) * lax.axis_size(FSDP)
    average = reward_sum[0] / rollout_count
    variance = square_sum[0] / rollout_count - average * average
    grad_scale = lax.rsqrt(variance + EPSILON) * lax.rsqrt(token_total[0])
    coefficient = live_flag.astype(jnp.float32) * (reward_value[0] - average) * grad_scale
    work_unit, work_normed, work_cotangent, work_live = (
        unit_rows,
        normed,
        seq_cotangent,
        live_flag,
    )
    grad_weight, grad_gain = accumulate(
        work_unit, work_normed, work_cotangent, coefficient, work_live, weight_full
    )
    shares = in_one_piece((grad_weight, grad_gain), FSDP, 0, 1)
    weight_grad, gain_grad = (
        total_of_pieces(shares[0], REPLICA),
        total_of_pieces(shares[1], REPLICA),
    )
    return (key_values, weight_grad, gain_grad)


def solution(mesh):
    torus = Mesh(mesh.devices.reshape(8, 2, 8, 8), ("replica_0", "replica_1", "fsdp_0", "fsdp_1"))
    return jax.shard_map(
        shards,
        mesh=torus,
        in_specs=(
            P(REPLICA_FSDP, None, None),
            P(REPLICA_FSDP, None, None),
            P(FSDP, None),
            P(FSDP),
            P(REPLICA_FSDP),
            P(REPLICA_FSDP),
            P(REPLICA_FSDP),
        ),
        out_specs=(P(REPLICA_FSDP, None, None), P(FSDP, None), P(FSDP)),
        check_vma=False,
    )
```

profile of v0, /device:TPU:1, one launch (start us, length us, event | category | flops | bytes accessed | tf_op | source)
XLA Modules:
  0.0 487.0 jit_solution(16312085735451792389)
XLA Ops:
  10.8 27.2 %all-reduce.3 = (f32[1]{0:T(128)}, f32[1]{0:T(128)}, f32[1]{0:T(128)}) all-reduce(f32[1]{0:T(128)S(6)} %mul.64, f32[1]{0:T(128)S(6)} %convert_element_type.45, f32[1]{0:T(128)S(6)} %convert_element_type.46), channel_id=1, replica_groups=mesh['replica_0'=8,'replica_1'=2,'fsdp_0'=8,'fsdp_1'=8] {'replica_0'}, use_global_device_ids=true, to_apply=%region_7.0 | all-reduce | flops 3 | bytes 24 | tf_op jit(solution)/shard_map/psum | solution.py:32
  38.0 7.2 %all-reduce.4 = (f32[1]{0:T(128)}, f32[1]{0:T(128)}, f32[1]{0:T(128)}) all-reduce(f32[1]{0:T(128)} %get-tuple-element.80, f32[1]{0:T(128)} %get-tuple-element.81, f32[1]{0:T(128)} %get-tuple-element.82), channel_id=1, replica_groups=mesh['replica_0'=8,'replica_1'=2,'fsdp_0'=8,'fsdp_1'=8] {'replica_1'}, use_global_device_ids=true, to_apply=%region_8.0 | all-reduce | flops 3 | bytes 24 | tf_op jit(solution)/shard_map/psum | solution.py:32
  45.3 14.4 %all-reduce.2 = (f32[1]{0:T(128)}, f32[1]{0:T(128)}, f32[1]{0:T(128)}) all-reduce(f32[1]{0:T(128)} %get-tuple-element.83, f32[1]{0:T(128)} %get-tuple-element.84, f32[1]{0:T(128)} %get-tuple-element.85), channel_id=1, replica_groups=mesh['replica_0'=8,'replica_1'=2,'fsdp_0'=8,'fsdp_1'=8] {'fsdp_0'}, use_global_device_ids=true, to_apply=%region_9.0 | all-reduce | flops 3 | bytes 24 | tf_op jit(solution)/shard_map/psum | solution.py:32
  59.7 15.5 %all-reduce.1 = (f32[1]{0:T(128)}, f32[1]{0:T(128)}, f32[1]{0:T(128)}) all-reduce(f32[1]{0:T(128)} %get-tuple-element.77, f32[1]{0:T(128)} %get-tuple-element.78, f32[1]{0:T(128)} %get-tuple-element.79), channel_id=1, replica_groups=mesh['replica_0'=8,'replica_1'=2,'fsdp_0'=8,'fsdp_1'=8] {'fsdp_1'}, use_global_device_ids=true, to_apply=%region_10.0 | all-reduce | flops 3 | bytes 24 | tf_op jit(solution)/shard_map/psum | solution.py:32
  80.3 3.2 sort.17
  83.5 1.9 gather_fusion.1
  87.8 21.8 %all-gather.5.cloned.1.call-done = bf16[2048,513]{1,0:T(8,128)(2,1)} async-done(((bf16[32,513]{1,0:T(8,128)(2,1)}), bf16[2048,513]{1,0:T(8,128)(2,1)}) %all-gather.5.cloned.1.call-update) | async-done | bytes 2101264 | tf_op jit(solution)/shard_map/all_gather | solution.py:24
  111.0 1.5 convert_multiply_fusion
  112.6 2.3 gather_fusion
  114.9 2.4 broadcast_select_fusion.1
  117.3 2.7 gather_fusion.3
  120.0 3.1 broadcast_select_fusion
  123.2 2.5 broadcast_in_dim.49
  125.7 13.7 %while.12 = (s32[]{:T(128)}, f32[2048,512]{1,0:T(8,128)}, f32[2048]{0:T(1024)S(1)}, s32[]{:T(128)}, bf16[256,2048]{1,0:T(8,128)(2,1)}, /*index=5*/f32[256]{0:T(2...) while((s32[]{:T(128)}, f32[2048,512]{1,0:T(8,128)}, ...), condition=%wide.region_17.18_spmd, body=%wide.region_15.17_spmd.sunk | while | flops 135495680 | bytes 10980023 | solution.py:88
  125.8 5.1 %convolution_add_fusion.2 = f32[2048,512]{1,0:T(8,128)} fusion(f32[2048,512]{1,0:T(8,128)} %get-tuple-element.162, bf16[256,2048]{1,0:T(8,128)(2,1)} %get-tuple-element.178, s32[]{:T(128)S(6)} %select_n.53, bf16[256,512]{1,0:T(8,128)(2,1)} %get-tuple-element.180, f32[32]{0:T(128)S(1)} %dynamic_slice.27), kind=kOutput, calls=%fused_computation.4.clone.1 | convolution fusion | flops 68206592 | bytes 8553600 | tf_op jit(solution)/shard_map/while/body/td,tk->dk/dot_general | solution.py:79
  130.8 1.7 fusion.16
  132.6 5.1 %convolution_add_fusion.2 = f32[2048,512]{1,0:T(8,128)} fusion(f32[2048,512]{1,0:T(8,128)} %get-tuple-element.162, bf16[256,2048]{1,0:T(8,128)(2,1)} %get-tuple-element.178, s32[]{:T(128)S(6)} %select_n.53, bf16[256,512]{1,0:T(8,128)(2,1)} %get-tuple-element.180, f32[32]{0:T(128)S(1)} %dynamic_slice.27), kind=kOutput, calls=%fused_computation.4.clone.1 | convolution fusion | flops 68206592 | bytes 8553600 | tf_op jit(solution)/shard_map/while/body/td,tk->dk/dot_general | solution.py:79
  137.7 1.7 fusion.16
  139.8 5.0 %pad_maximum_fusion = f32[2048,513]{1,0:T(8,128)} fusion(f32[2048,1]{1,0:T(8,128)S(1)} %copy.14, f32[2048,512]{1,0:T(8,128)} %get-tuple-element.54), kind=kLoop, calls=%fused_computation.11 | loop fusion | flops 1050624 | bytes 8404992 | tf_op jit(solution)/shard_map/concatenate | solution.py:37
  144.9 280.6 %reduce-scatter.2.cloned.1.call-done = f32[32,513]{1,0:T(8,128)} async-done(((f32[2048,513]{1,0:T(8,128)}), f32[32,513]{1,0:T(8,128)}) %reduce-scatter.2.cloned.1.call-update) | async-done | bytes 65680 | tf_op jit(solution)/shard_map/reduce_scatter | solution.py:40
  428.9 3.0 fusion.5
  433.0 30.9 %all-reduce = f32[512]{0:T(512)S(1)} all-reduce(f32[512]{0:T(512)S(1)} %dynamic-update-slice), channel_id=3, replica_groups=mesh['replica_0'=8,'replica_1'=2,'fsdp_0'=8,'fsdp_1'=8] {'replica_0','re..., use_global_device_ids=true, to_apply=%add | all-reduce | flops 512 | bytes 4096
  464.5 14.0 %all-gather.7.cloned.1.call-done = f32[512,512]{1,0:T(8,128)} async-done(((f32[32,512]{1,0:T(8,128)}), f32[512,512]{1,0:T(8,128)}) %all-gather.7.cloned.1.call-update) | async-done | bytes 1048592 | tf_op jit(solution)/shard_map/all_gather | solution.py:48
  478.5 1.9 reduce_sum.47
  (38 shorter events, 11.7 us)
Async XLA Ops:
  7.2 78.3 %copy-start = (bf16[1,256,512]{2,1,0:T(8,128)(2,1)S(1)}, bf16[1,256,512]{2,1,0:T(8,128)(2,1)}, u32[]{:S(2)}) copy-start(bf16[1,256,512]{2,1,0:T(8,128)(2,1)} %param.10) | copy-start | bytes 786436
  7.2 79.5 %copy-start.1 = (bf16[1,256,2048]{2,1,0:T(8,128)(2,1)S(1)}, bf16[1,256,2048]{2,1,0:T(8,128)(2,1)}, u32[]{:S(2)}) copy-start(bf16[1,256,2048]{2,1,0:T(8,128)(2,1)} %param.9) | copy-start | bytes 3145732
  7.2 102.4 %all-gather.5.cloned.1.call-start = ((), (), s32[]{:S(2)}) async-start(), calls=%async_computation.1 | async-start | bytes 2662400 | tf_op jit(solution)/shard_map/all_gather | solution.py:24
  9.5 416.0 %reduce-scatter.2.cloned.1.call-start = ((), (), s32[]{:S(2)}) async-start(), calls=%async_computation.2 | async-start | bytes 5324800 | tf_op jit(solution)/shard_map/reduce_scatter | solution.py:40
  123.2 2.6 slice-start
  144.8 333.7 %all-gather.7.cloned.1.call-start = ((), (), s32[]{:S(2)}) async-start(), calls=%async_computation.3 | async-start | bytes 1114112 | tf_op jit(solution)/shard_map/all_gather | solution.py:48
Sparse Core Ops, SparseCore 0:
  12.8 96.7 all-gather.4
  144.9 280.4 reduce-scatter.1
  428.8 49.6 all-gather.6
where the time goes:
time: 488 us; the launch traced here: 487 us
  waiting for transfers between devices  316 us (65%)
  blocking collectives  95.3 us (20%)
  other arithmetic  22.2 us (5%)
  between operations  20.4 us (4%)
  matrix products  16.5 us (3%)
  local copies, waits for them, and re-layouts  16 us (3%)
    reduce_scatter x1, waiting for transfers between devices, in_one_piece(): filled = lax.psum_scatter(both, axis, scatter_dimension=dim, tiled=True)  281 us
    psum x4, blocking collectives, over_axes(): return functools.reduce(lax.psum, axes, value)  64.3 us
    unnamed x1, blocking collectives  30.9 us
    all_gather x1, waiting for transfers between devices, side_by_side(): filled = lax.all_gather(both, axis, axis=dim, tiled=True)  21.8 us
    all_gather x1, waiting for transfers between devices, total_of_pieces(): pieces = lax.all_gather(value, axis)  14 us
    dot_general x2, matrix products, one_block(): jnp.einsum('td,tk->dk', normed_part, weighted, preferred_element_type=jnp...  10.1 us
  transfers between devices with their start and end apart: 3, of which 3 were waited for; matrix products, arithmetic and copies ran while one was open for 3% of the time, Pallas kernels for 0%

commit v1 on v0

v1 whole, which is shorter than its diff:
```python
import jax
import jax.numpy as jnp
from jax import lax
from jax.sharding import Mesh
from jax.sharding import PartitionSpec as P

CORE, Z, X, Y = "core", "z", "x", "y"
REPLICA = (Z, CORE)
FSDP = (X, Y)
ALL = (Z, CORE, X, Y)
EPSILON = 1e-06


def from_all(value, axes):
    count = lax.axis_size(axes)
    copies = jnp.broadcast_to(value[None], (count, *value.shape))
    return lax.all_to_all(copies, axes, 0, 0, tiled=True)


def shards(states, cotangent, kv_weight, norm_gain, prompt_len, response_len, reward_bucket):
    fsdp, replicas = lax.axis_size(FSDP), lax.axis_size(REPLICA)
    rows_own, features = kv_weight.shape
    rows_half = rows_own // 2
    seq, width = states.shape[1:]
    weight_full = lax.all_gather(kv_weight, FSDP, axis=0, tiled=True)

    reward = reward_bucket.astype(jnp.float32)
    stats = jnp.concatenate([reward, reward * reward, response_len.astype(jnp.float32)])
    stats = from_all(jnp.pad(stats, (0, 125)), REPLICA).sum(axis=0)[:3]
    gain_own = norm_gain.astype(jnp.float32)
    mixed = jnp.concatenate([gain_own, stats, jnp.zeros((128 - rows_own - 3,), jnp.float32)])
    mixed = from_all(mixed, FSDP)
    gain_full = mixed[:, :rows_own].reshape(width)
    reward_sum, square_sum, token_total = mixed[:, rows_own : rows_own + 3].sum(axis=0)
    count = fsdp * replicas
    average = reward_sum / count
    variance = square_sum / count - average * average
    grad_scale = lax.rsqrt(variance + EPSILON) * lax.rsqrt(token_total)
    scale_own = (reward[0] - average) * grad_scale

    widened = states[0].astype(jnp.float32)
    unit = widened * lax.rsqrt(jnp.mean(widened * widened, axis=-1, keepdims=True) + EPSILON)
    position = jnp.arange(seq, dtype=jnp.int32)
    live = (position >= prompt_len[0]) & (position < prompt_len[0] + response_len[0])
    masked = jnp.where(live[:, None], cotangent[0], jnp.zeros((), cotangent.dtype))
    product = jnp.einsum(
        "td,tk->dk", unit.astype(jnp.bfloat16), masked, preferred_element_type=jnp.float32
    )
    scaled = (product * scale_own).astype(jnp.bfloat16)
    halves = scaled.reshape(fsdp, 2, rows_half, features)
    halves = halves.transpose(1, 0, 2, 3)

    pair = lax.all_to_all(halves, CORE, 0, 0, tiled=True)
    chip = pair.astype(jnp.float32).sum(axis=0).astype(jnp.bfloat16)
    plane = lax.all_to_all(chip, FSDP, 0, 0, tiled=True)
    plane = plane.astype(jnp.float32).sum(axis=0)
    every = from_all(plane, REPLICA).reshape(replicas // 2, 2, rows_half, features)
    total = every.sum(axis=0).reshape(rows_own, features)

    grad_weight = total * (1.0 + gain_own)[:, None]
    grad_gain = jnp.sum(total * kv_weight.astype(jnp.float32), axis=1)

    normed = (unit * (1.0 + gain_full)).astype(jnp.bfloat16)
    key_values = jnp.dot(normed, weight_full, preferred_element_type=jnp.float32)
    return (key_values.astype(jnp.bfloat16)[None], grad_weight, grad_gain)


def solution(mesh):
    torus = Mesh(mesh.devices.reshape(8, 2, 8, 8), ALL)
    split = (Z, CORE, X, Y)
    return jax.shard_map(
        shards,
        mesh=torus,
        in_specs=(
            P(split, None, None),
            P(split, None, None),
            P(FSDP, None),
            P(FSDP),
            P(split),
            P(split),
            P(split),
        ),
        out_specs=(P(split, None, None), P(FSDP, None), P(FSDP)),
        check_vma=False,
    )
```

time: 488 us -> 147 us (0.30)
  the two profiles are of different devices: /device:TPU:1 before, /device:TPU:4 now
where the time goes in v1:
time: 147 us
  blocking collectives  41.8 us (28%)
  waiting for transfers between devices  38.8 us (26%)
  starting transfers between devices  33.9 us (23%)
  between operations  19.4 us (13%)
  matrix products  5.17 us (4%)
  other arithmetic  4.58 us (3%)
  local copies, waits for them, and re-layouts  2.99 us (2%)
    all_to_all x1, blocking collectives, shards(): plane = lax.all_to_all(chip, FSDP, 0, 0, tiled=True)  36.4 us
    all_to_all x3, starting transfers between devices, from_all(): return lax.all_to_all(copies, axes, 0, 0, tiled=True)  33.9 us
    all_to_all x3, waiting for transfers between devices, from_all(): return lax.all_to_all(copies, axes, 0, 0, tiled=True)  29.9 us
    all_gather x1, waiting for transfers between devices, shards(): weight_full = lax.all_gather(kv_weight, FSDP, axis=0, tiled=True)  8.22 us
    all_to_all x1, blocking collectives, shards(): pair = lax.all_to_all(halves, CORE, 0, 0, tiled=True)  5.42 us
    dot_general x1, matrix products, shards(): jnp.dot(normed, weight_full, preferred_element_type=jnp.float32)  3.06 us
  transfers between devices with their start and end apart: 4, of which 4 were waited for; matrix products, arithmetic and copies ran while one was open for 6% of the time, Pallas kernels for 0%

profile of v1, /device:TPU:4, one launch (start us, length us, event | category | flops | bytes accessed | tf_op | source)
XLA Modules:
  0.0 146.7 jit_solution(3323260437154657482)
XLA Ops:
  8.5 0.1 select_maximum_fusion
  8.5 0.6 broadcast_in_dim.22
  9.1 16.8 %all-to-all-start = ((f32[16,1,128]{2,1,0:T(1,128)}), f32[16,1,128]{2,1,0:T(1,128)S(1)}, u32[]{:S(2)}, u32[]{:S(2)}) async-start(f32[16,1,128]{2,1,0:T(1,128)} %broadcast_in_dim.22), calls=%async_computation | async-start | bytes 16384 | tf_op jit(solution)/shard_map/all_to_all | solution.py:17
  26.0 0.7 all-gather.2.cloned.1.call-update
  26.7 1.5 %fusion.2 = f32[256]{0:T(256)S(1)} fusion(bf16[1,256,2048]{2,1,0:T(8,128)(2,1)} %param.7), kind=kLoop, calls=%fused_computation.5 | loop fusion | flops 1572608 | bytes 1049600 | tf_op jit(solution)/shard_map/reduce_sum | solution.py:42
  28.2 0.7 convert_element_type.45
  29.5 4.0 %all-to-all-done = f32[16,1,128]{2,1,0:T(1,128)S(1)} async-done(((f32[16,1,128]{2,1,0:T(1,128)}), f32[16,1,128]{2,1,0:T(1,128)S(1)}, u32[]{:S(2)}, u32[]{:S(2)}) %all-to-all-start) | async-done | bytes 8224 | tf_op jit(solution)/shard_map/all_to_all | solution.py:17
  33.6 0.6 broadcast_in_dim.24
  34.2 13.5 %all-to-all-start.1 = ((f32[64,1,128]{2,1,0:T(1,128)}), f32[64,1,128]{2,1,0:T(1,128)S(1)}, u32[]{:S(2)}, u32[]{:S(2)}) async-start(f32[64,1,128]{2,1,0:T(1,128)} %broadcast_in_dim.24), calls=%async_computation.1 | async-start | bytes 65536 | tf_op jit(solution)/shard_map/all_to_all | solution.py:17
  47.8 10.1 %all-to-all-done.1 = f32[64,1,128]{2,1,0:T(1,128)S(1)} async-done(((f32[64,1,128]{2,1,0:T(1,128)}), f32[64,1,128]{2,1,0:T(1,128)S(1)}, u32[]{:S(2)}, u32[]{:S(2)}) %all-to-all-start.1) | async-done | bytes 32800 | tf_op jit(solution)/shard_map/all_to_all | solution.py:17
  57.9 0.1 slice_reduce_fusion
  58.0 0.6 fusion.19
  61.9 2.1 %multiply_convert_fusion = bf16[2048,512]{1,0:T(8,128)(2,1)S(1)} fusion(f32[]{:T(128)} %bitcast.8, bf16[1,256,2048]{2,1,0:T(8,128)(2,1)} %param.7, f32[256]{0:T(256)S(1)} %add_rsqrt_fusion, bf16[1,256,512]{2,1,0:T(8,128)(2,1)} %param.8, pred[256]{0:T(512)(128)(4,1)S(1)} %compare_and_fusion), kind=kOutput, calls=%fused_computation | convolution fusion | flops 540672000 | bytes 3409156 | tf_op jit(solution)/shard_map/td,tk->dk/dot_general | solution.py:46
  64.0 0.2 copy.15
  64.2 5.4 %all_to_all.30 = bf16[2,64,16,512]{3,2,1,0:T(8,128)(2,1)S(1)} all-to-all(bf16[2,64,16,512]{3,2,1,0:T(8,128)(2,1)S(1)} %bitcast.41), channel_id=1, replica_groups=mesh['z'=8,'core'=2,'x'=8,'y'=8] {'core'}, dimensions={0} | all-to-all | bytes 4194304 | tf_op jit(solution)/shard_map/all_to_all | solution.py:53
  69.7 0.6 reduce_sum.69
  70.3 36.4 %all_to_all.31 = bf16[64,16,512]{2,1,0:T(8,128)(2,1)S(1)} all-to-all(bf16[64,16,512]{2,1,0:T(8,128)(2,1)S(1)} %reduce_sum.69), channel_id=1, replica_groups=mesh['z'=8,'core'=2,'x'=8,'y'=8] {'x','y'}, dimensions={0} | all-to-all | bytes 2097152 | tf_op jit(solution)/shard_map/all_to_all | solution.py:55
  106.6 0.2 convert_reduce_fusion
  106.8 0.9 broadcast_in_dim.46
  107.7 3.6 %all-to-all-start.4 = ((f32[16,16,512]{2,1,0:T(8,128)}), f32[16,16,512]{2,1,0:T(8,128)S(1)}, u32[]{:S(2)}, u32[]{:S(2)}) async-start(f32[16,16,512]{2,1,0:T(8,128)} %broadcast_in_dim.46), calls=%async_computation.4 | async-start | bytes 1048576 | tf_op jit(solution)/shard_map/all_to_all | solution.py:17
  111.4 15.8 %all-to-all-done.4 = f32[16,16,512]{2,1,0:T(8,128)S(1)} async-done(((f32[16,16,512]{2,1,0:T(8,128)}), f32[16,16,512]{2,1,0:T(8,128)S(1)}, u32[]{:S(2)}, u32[]{:S(2)}) %all-to-all-start.4) | async-done | bytes 524320 | tf_op jit(solution)/shard_map/all_to_all | solution.py:17
  127.2 1.3 fusion.17
  128.5 8.2 %all-gather.2.cloned.1.call-done = bf16[2048,512]{1,0:T(8,128)(2,1)} async-done(((bf16[32,512]{1,0:T(8,128)(2,1)}), bf16[2048,512]{1,0:T(8,128)(2,1)}) %all-gather.2.cloned.1.call-update) | async-done | bytes 2097168 | tf_op jit(solution)/shard_map/all_gather | solution.py:25
  136.8 3.1 %fusion.6 = bf16[1,256,512]{2,1,0:T(8,128)(2,1)} fusion(bf16[2048,512]{1,0:T(8,128)(2,1)} %all-gather.2.cloned.1.call-done, bf16[1,256,2048]{2,1,0:T(8,128)(2,1)S(1)} %copy-done, f32[2048]{0:T(1024)S(1)} %add.45, f32[256]{0:T(256)S(1)} %add_rsqrt_fusion), kind=kOutput, calls=%fused_computation.12 | convolution fusion | flops 539099136 | bytes 3417088 | tf_op jit(solution)/shard_map/dot_general | solution.py:64
  (16 shorter events, 0.3 us)
Async XLA Ops:
  9.1 24.3 %all-to-all-start = ((f32[16,1,128]{2,1,0:T(1,128)}), f32[16,1,128]{2,1,0:T(1,128)S(1)}, u32[]{:S(2)}, u32[]{:S(2)}) async-start(f32[16,1,128]{2,1,0:T(1,128)} %broadcast_in_dim.22), calls=%async_computation | async-start | bytes 16384 | tf_op jit(solution)/shard_map/all_to_all | solution.py:17
  25.9 110.8 %all-gather.2.cloned.1.call-start = ((), (), s32[]{:S(2)}) async-start(), calls=%async_computation.5 | async-start | bytes 2129920 | tf_op jit(solution)/shard_map/all_gather | solution.py:25
  34.2 23.7 %all-to-all-start.1 = ((f32[64,1,128]{2,1,0:T(1,128)}), f32[64,1,128]{2,1,0:T(1,128)S(1)}, u32[]{:S(2)}, u32[]{:S(2)}) async-start(f32[64,1,128]{2,1,0:T(1,128)} %broadcast_in_dim.24), calls=%async_computation.1 | async-start | bytes 65536 | tf_op jit(solution)/shard_map/all_to_all | solution.py:17
  70.2 41.0 %copy-start.2 = (bf16[32]{0:T(256)(128)(2,1)S(1)}, bf16[32]{0:T(256)(128)(2,1)}, u32[]{:S(2)}) copy-start(bf16[32]{0:T(256)(128)(2,1)} %param.10) | copy-start | bytes 196
  106.6 20.6 %copy-start.1 = (bf16[32,512]{1,0:T(8,128)(2,1)S(1)}, bf16[32,512]{1,0:T(8,128)(2,1)}, u32[]{:S(2)}) copy-start(bf16[32,512]{1,0:T(8,128)(2,1)} %param.9) | copy-start | bytes 98308
  106.6 30.1 %copy-start = (bf16[1,256,2048]{2,1,0:T(8,128)(2,1)S(1)}, bf16[1,256,2048]{2,1,0:T(8,128)(2,1)}, u32[]{:S(2)}) copy-start(bf16[1,256,2048]{2,1,0:T(8,128)(2,1)} %param.7) | copy-start | bytes 3145732
  107.7 19.5 %all-to-all-start.4 = ((f32[16,16,512]{2,1,0:T(8,128)}), f32[16,16,512]{2,1,0:T(8,128)S(1)}, u32[]{:S(2)}, u32[]{:S(2)}) async-start(f32[16,16,512]{2,1,0:T(8,128)} %broadcast_in_dim.46), calls=%async_computation.4 | async-start | bytes 1048576 | tf_op jit(solution)/shard_map/all_to_all | solution.py:17
Sparse Core Ops, SparseCore 0:
  30.9 105.7 all-gather.1

commit v2 on v1

v2 whole, which is shorter than its diff:
```python
import jax
import jax.numpy as jnp
from jax import lax
from jax.sharding import Mesh
from jax.sharding import PartitionSpec as P

CORE, Z, X, Y = "core", "z", "x", "y"
REPLICA = (Z, CORE)
FSDP = (X, Y)
ALL = (Z, CORE, X, Y)
EPSILON = 1e-06
SWAP = ((0, 1), (1, 0))
LANES = 128
DIGIT = 64.0


def from_all(value, axes):
    count = lax.axis_size(axes)
    copies = jnp.broadcast_to(value[None], (count, *value.shape))
    return lax.all_to_all(copies, axes, 0, 0, tiled=True)


def half_of(value, which):
    half = value.shape[-1] // 2
    return lax.dynamic_slice_in_dim(value, which * half, half, value.ndim - 1)


def side_by_side(mine, other, core):
    left = jnp.where(core == 0, mine, other)
    right = jnp.where(core == 0, other, mine)
    return jnp.concatenate([left, right], axis=-1)


def shards(states, cotangent, kv_weight, norm_gain, prompt_len, response_len, reward_bucket):
    fsdp, replicas = lax.axis_size(FSDP), lax.axis_size(REPLICA)
    core = lax.axis_index(CORE)
    rows_own, features = kv_weight.shape
    seq, width = states.shape[1:]
    with jax.named_scope("column"):
        reward = reward_bucket.astype(jnp.float32)
        stats = jnp.concatenate([reward, reward * reward, response_len.astype(jnp.float32)])
        stats = from_all(jnp.pad(stats, (0, LANES - 3)), REPLICA)
    reward_other = stats[2 * lax.axis_index(Z) + 1 - core, 0]
    stats = stats.sum(axis=0)
    square_high, token_high = jnp.floor(stats[1:3] / DIGIT)
    square_low, token_low = stats[1] - DIGIT * square_high, stats[2] - DIGIT * token_high
    digits = jnp.stack([stats[0], square_high, square_low, token_high, token_low])
    tail = jnp.concatenate([norm_gain, digits.astype(jnp.bfloat16)])
    tail = jnp.pad(tail, (0, LANES - tail.shape[0]))[None]
    weight_own = half_of(kv_weight, core)
    lane_tiles = weight_own.shape[-1] // LANES
    weight_own = [weight_own[:, k * LANES : (k + 1) * LANES] for k in range(lane_tiles)]
    with jax.named_scope("weight"):
        filled = from_all(jnp.concatenate([*weight_own, tail]), FSDP)
    weight_mine = jnp.concatenate(
        [
            filled[:, k * rows_own : (k + 1) * rows_own].reshape(width, LANES)
            for k in range(lane_tiles)
        ],
        axis=-1,
    )
    filled = filled[:, lane_tiles * rows_own].astype(jnp.float32)
    gain_own = norm_gain.astype(jnp.float32)
    gain_full = filled[:, :rows_own].reshape(width)
    digits = filled[:, rows_own : rows_own + 5].sum(axis=0)
    count = fsdp * replicas
    average = digits[0] / count
    variance = (DIGIT * digits[1] + digits[2]) / count - average * average
    token_total = DIGIT * digits[3] + digits[4]
    grad_scale = lax.rsqrt(variance + EPSILON) * lax.rsqrt(token_total)

    widened = states[0].astype(jnp.float32)
    unit = widened * lax.rsqrt(jnp.mean(widened * widened, axis=-1, keepdims=True) + EPSILON)
    coarse = lax.reduce_precision(unit, 8, 7)
    fine = (unit - coarse).astype(jnp.bfloat16)
    coarse = coarse.astype(jnp.bfloat16)
    position = jnp.arange(seq, dtype=jnp.int32)
    live = (position >= prompt_len[0]) & (position < prompt_len[0] + response_len[0])
    masked = jnp.where(live[:, None], cotangent[0], jnp.zeros((), cotangent.dtype))

    def product(part):
        def with_unit(rows):
            return jnp.einsum("td,tk->dk", rows, part, preferred_element_type=jnp.float32)

        return with_unit(coarse) + with_unit(fine)

    sent = product(half_of(masked, 1 - core)).astype(jnp.bfloat16)
    got = lax.ppermute(sent, CORE, SWAP)
    kept = lax.optimization_barrier(product(half_of(masked, core)))

    chip = (reward[0] - average) * kept + (reward_other - average) * got.astype(jnp.float32)
    chip = chip.astype(jnp.bfloat16).reshape(fsdp, rows_own, features // 2)
    plane = lax.all_to_all(chip, FSDP, 0, 0, tiled=True)
    plane = plane.astype(jnp.float32).sum(axis=0)
    mine = from_all(plane, Z).sum(axis=0) * grad_scale
    total = side_by_side(mine, lax.ppermute(mine, CORE, SWAP), core)

    grad_weight = total * (1.0 + gain_own)[:, None]
    grad_gain = jnp.sum(total * kv_weight.astype(jnp.float32), axis=1)

    normed = (unit * (1.0 + gain_full)).astype(jnp.bfloat16)
    weight_other = lax.ppermute(weight_mine, CORE, SWAP)

    def projected(weight):
        result = jnp.dot(normed, weight, preferred_element_type=jnp.float32)
        return result.astype(jnp.bfloat16)

    key_values = side_by_side(projected(weight_mine), projected(weight_other), core)
    return (key_values[None], grad_weight, grad_gain)


def solution(mesh):
    torus = Mesh(mesh.devices.reshape(8, 2, 8, 8), ALL)
    return jax.shard_map(
        shards,
        mesh=torus,
        in_specs=(
            P(ALL, None, None),
            P(ALL, None, None),
            P(FSDP, None),
            P(FSDP),
            P(ALL),
            P(ALL),
            P(ALL),
        ),
        out_specs=(P(ALL, None, None), P(FSDP, None), P(FSDP)),
        check_vma=False,
    )
```

time: 147 us -> 143 us (0.973)
  the two profiles are of different devices: /device:TPU:4 before, /device:TPU:1 now
where the time goes in v2:
time: 143 us; the launch traced here: 142 us
  starting transfers between devices  57.5 us (40%)
  waiting for transfers between devices  50.9 us (36%)
  between operations  11.9 us (8%)
  local copies, waits for them, and re-layouts  8.71 us (6%)
  other arithmetic  6.79 us (5%)
  matrix products  6.16 us (4%)
    all_to_all x3, starting transfers between devices, from_all(): return lax.all_to_all(copies, axes, 0, 0, tiled=True)  35 us
    all_to_all x3, waiting for transfers between devices, from_all(): return lax.all_to_all(copies, axes, 0, 0, tiled=True)  34.2 us
    all_to_all x1, waiting for transfers between devices, shards(): plane = lax.all_to_all(chip, FSDP, 0, 0, tiled=True)  16.7 us
    all_to_all x1, starting transfers between devices, shards(): plane = lax.all_to_all(chip, FSDP, 0, 0, tiled=True)  9.17 us
    ppermute x1, starting transfers between devices, shards(): total = side_by_side(mine, lax.ppermute(mine, CORE, SWAP), core)  7.17 us
    dot_general x4, matrix products, with_unit(): jnp.einsum('td,tk->dk', rows, part, preferred_element_type=jnp.float32)  3.6 us
    ppermute x1, starting transfers between devices, shards(): weight_other = lax.ppermute(weight_mine, CORE, SWAP)  3.31 us
  transfers between devices with their start and end apart: 7, of which 4 were waited for; matrix products, arithmetic and copies ran while one was open for 10% of the time, Pallas kernels for 0%

profile of v2, /device:TPU:1, one launch (start us, length us, event | category | flops | bytes accessed | tf_op | source)
XLA Modules:
  0.0 142.0 jit_solution(18277142683329020532)
XLA Ops:
  2.7 18.2 %all-to-all-start = ((f32[16,1,128]{2,1,0:T(1,128)}), f32[16,1,128]{2,1,0:T(1,128)S(1)}, u32[]{:S(2)}, u32[]{:S(2)}) async-start(f32[16,1,128]{2,1,0:T(1,128)} %broadcast_in_dim.22), calls=%async_computation | async-start | bytes 16384 | tf_op jit(solution)/shard_map/column/all_to_all | solution.py:20
  20.9 0.7 constant_dynamic-slice_fusion
  21.6 6.3 %all-to-all-done = f32[16,1,128]{2,1,0:T(1,128)S(1)} async-done(((f32[16,1,128]{2,1,0:T(1,128)}), f32[16,1,128]{2,1,0:T(1,128)S(1)}, u32[]{:S(2)}, u32[]{:S(2)}) %all-to-all-start) | async-done | bytes 8224 | tf_op jit(solution)/shard_map/column/all_to_all | solution.py:20
  32.9 0.8 concatenate.20
  33.7 1.2 broadcast_in_dim.24
  34.9 13.4 %all-to-all-start.1 = ((bf16[64,65,128]{2,1,0:T(8,128)(2,1)}), bf16[64,65,128]{2,1,0:T(8,128)(2,1)}, u32[]{:S(2)}, u32[]{:S(2)}) async-start(bf16[64,65,128]{2,1,0:T(8,128)(2,1)} %broadcast_in_dim.24), calls=%async_computation.1 | async-start | bytes 2359296 | tf_op jit(solution)/shard_map/weight/all_to_all | solution.py:20
  50.1 1.7 %fusion.1 = bf16[2048,256]{1,0:T(8,128)(2,1)} fusion(f32[2048,256]{1,0:T(8,128)S(1)} %fusion.5, bf16[1,256,2048]{2,1,0:T(8,128)(2,1)S(1)} %copy-done, f32[256]{0:T(256)S(1)} %add_rsqrt_fusion, bf16[256,512]{1,0:T(8,128)(2,1)S(1)} %bitcast_select_fusion, s32[]{:T(128)S(6)} %select_n.45), kind=kOutput, calls=%fused_computation.7 | convolution fusion | flops 272105472 | bytes 4326404 | tf_op jit(solution)/shard_map/td,tk->dk/dot_general | solution.py:83
  51.7 2.8 %collective-permute-start.1 = (bf16[2048,256]{1,0:T(8,128)(2,1)}, bf16[2048,256]{1,0:T(8,128)(2,1)}, u32[]{:S(2)}, u32[]{:S(2)}) collective-permute-start(bf16[2048,256]{1,0:T(8,128)(2,1)} %fusion.1), channel_id=1, source_target_pairs={{0,64},{64,0},{1,65},{65,1},{2,66},{66,2},{3,67},{67,3},{4,68},{68... | collective-permute-start | bytes 3145736 | tf_op jit(solution)/shard_map/ppermute | solution.py:88
  56.4 21.2 %all-to-all-done.1 = bf16[64,65,128]{2,1,0:T(8,128)(2,1)} async-done(((bf16[64,65,128]{2,1,0:T(8,128)(2,1)}), bf16[64,65,128]{2,1,0:T(8,128)(2,1)}, u32[]{:S(2)}, u32[]{:S(2)}) %all-to-all-start.1) | async-done | bytes 1064992 | tf_op jit(solution)/shard_map/weight/all_to_all | solution.py:20
  77.7 0.9 slice_convert_fusion
  78.7 0.7 fusion.21
  80.7 2.5 %add_convert_fusion = bf16[2048,256]{1,0:T(8,128)(2,1)} fusion(bf16[2048,256]{1,0:T(8,128)(2,1)} %collective-permute-done.1, f32[2048,256]{1,0:T(8,128)S(1)} %convolution_add_fusion.1, f32[]{:T(128)S(6)} %sub.34, f32[]{:T(128)S(6)} %sub.31), kind=kLoop, calls=%fused_computation.12 | loop fusion | flops 2621440 | bytes 4194312 | tf_op jit(solution)/shard_map/convert_element_type | solution.py:92
  83.3 9.2 %all-to-all-start.2 = ((bf16[64,32,256]{2,1,0:T(8,128)(2,1)}), bf16[64,32,256]{2,1,0:T(8,128)(2,1)S(1)}, u32[]{:S(2)}, u32[]{:S(2)}) async-start(bf16[64,32,256]{2,1,0:T(8,128)(2,1)} %bitcast.36), calls=%async_computation.2 | async-start | bytes 2097152 | tf_op jit(solution)/shard_map/all_to_all | solution.py:93
  92.5 1.3 fusion.20
  93.8 1.1 pad_maximum_fusion
  94.8 3.3 %collective-permute-start = (bf16[2048,256]{1,0:T(8,128)(2,1)}, bf16[2048,256]{1,0:T(8,128)(2,1)}, u32[]{:S(2)}, u32[]{:S(2)}) collective-permute-start(bf16[2048,256]{1,0:T(8,128)(2,1)} %pad_maximum_fusion), channel_id=1, source_target_pairs={{0,64},{64,0},{1,65},{65,1},{2,66},{66,2},{3,67},{67,3},{4,68},{68... | collective-permute-start | bytes 3145736 | tf_op jit(solution)/shard_map/ppermute | solution.py:102
  102.3 16.7 %all-to-all-done.2 = bf16[64,32,256]{2,1,0:T(8,128)(2,1)S(1)} async-done(((bf16[64,32,256]{2,1,0:T(8,128)(2,1)}), bf16[64,32,256]{2,1,0:T(8,128)(2,1)S(1)}, u32[]{:S(2)}, u32[]{:S(2)}) %all-to-all-start.2) | async-done | bytes 1048608 | tf_op jit(solution)/shard_map/all_to_all | solution.py:93
  119.2 0.7 broadcast_in_dim.46
  119.9 3.4 %all-to-all-start.3 = ((f32[8,32,256]{2,1,0:T(8,128)}), f32[8,32,256]{2,1,0:T(8,128)S(1)}, u32[]{:S(2)}, u32[]{:S(2)}) async-start(f32[8,32,256]{2,1,0:T(8,128)} %broadcast_in_dim.46), calls=%async_computation.3 | async-start | bytes 524288 | tf_op jit(solution)/shard_map/all_to_all | solution.py:20
  124.0 1.9 %broadcast_select_fusion.1 = (bf16[256,256]{0,1:T(8,128)(2,1)S(1)}, bf16[256,256]{0,1:T(8,128)(2,1)S(1)}) fusion(bf16[256,256]{0,1:T(8,128)(2,1)S(1)} %convolution_convert_fusion.1, pred[]{:T(512)S(6)} %eq.2, bf16[2048,256]{1,0:T(8,128)(2,1)} %collective-permute-done, bf16[1,256,2048]{2,1,0:T(8,128)(2,1)S(1)} %copy-done, f32[2048]{0:T(1024)S(1)} %add.75, ...), kind=kOutput, calls=%fused_computation.21 | convolution fusion | flops 270729216 | bytes 2499585 | tf_op jit(solution)/shard_map/dot_general | solution.py:105
  125.9 6.7 %all-to-all-done.3 = f32[8,32,256]{2,1,0:T(8,128)S(1)} async-done(((f32[8,32,256]{2,1,0:T(8,128)}), f32[8,32,256]{2,1,0:T(8,128)S(1)}, u32[]{:S(2)}, u32[]{:S(2)}) %all-to-all-start.3) | async-done | bytes 262176 | tf_op jit(solution)/shard_map/all_to_all | solution.py:20
  132.6 7.2 %collective-permute-start.2 = (f32[32,256]{1,0:T(8,128)S(1)}, f32[32,256]{1,0:T(8,128)S(1)}, u32[]{:S(2)}, u32[]{:S(2)}) collective-permute-start(f32[32,256]{1,0:T(8,128)S(1)} %broadcast_multiply_fusion), channel_id=1, source_target_pairs={{0,64},{64,0},{1,65},{65,1},{2,66},{66,2},{3,67},{67,3},{4,68},{68... | collective-permute-start | bytes 98312 | tf_op jit(solution)/shard_map/ppermute | solution.py:96
  139.8 0.8 copy.15
  140.7 1.3 multiply_reduce_fusion
  (38 shorter events, 6.0 us)
Async XLA Ops:
  0.6 48.4 %copy-start = (bf16[1,256,2048]{2,1,0:T(8,128)(2,1)S(1)}, bf16[1,256,2048]{2,1,0:T(8,128)(2,1)}, u32[]{:S(2)}) copy-start(bf16[1,256,2048]{2,1,0:T(8,128)(2,1)} %param.7) | copy-start | bytes 3145732
  2.7 25.2 %all-to-all-start = ((f32[16,1,128]{2,1,0:T(1,128)}), f32[16,1,128]{2,1,0:T(1,128)S(1)}, u32[]{:S(2)}, u32[]{:S(2)}) async-start(f32[16,1,128]{2,1,0:T(1,128)} %broadcast_in_dim.22), calls=%async_computation | async-start | bytes 16384 | tf_op jit(solution)/shard_map/column/all_to_all | solution.py:20
  33.7 15.6 %copy-start.1 = (bf16[1,256,512]{2,1,0:T(8,128)(2,1)S(1)}, bf16[1,256,512]{2,1,0:T(8,128)(2,1)}, u32[]{:S(2)}) copy-start(bf16[1,256,512]{2,1,0:T(8,128)(2,1)} %param.8) | copy-start | bytes 786436
  34.9 42.8 %all-to-all-start.1 = ((bf16[64,65,128]{2,1,0:T(8,128)(2,1)}), bf16[64,65,128]{2,1,0:T(8,128)(2,1)}, u32[]{:S(2)}, u32[]{:S(2)}) async-start(bf16[64,65,128]{2,1,0:T(8,128)(2,1)} %broadcast_in_dim.24), calls=%async_computation.1 | async-start | bytes 2359296 | tf_op jit(solution)/shard_map/weight/all_to_all | solution.py:20
  51.7 29.0 %collective-permute-start.1 = (bf16[2048,256]{1,0:T(8,128)(2,1)}, bf16[2048,256]{1,0:T(8,128)(2,1)}, u32[]{:S(2)}, u32[]{:S(2)}) collective-permute-start(bf16[2048,256]{1,0:T(8,128)(2,1)} %fusion.1), channel_id=1, source_target_pairs={{0,64},{64,0},{1,65},{65,1},{2,66},{66,2},{3,67},{67,3},{4,68},{68... | collective-permute-start | bytes 3145736 | tf_op jit(solution)/shard_map/ppermute | solution.py:88
  83.3 35.7 %all-to-all-start.2 = ((bf16[64,32,256]{2,1,0:T(8,128)(2,1)}), bf16[64,32,256]{2,1,0:T(8,128)(2,1)S(1)}, u32[]{:S(2)}, u32[]{:S(2)}) async-start(bf16[64,32,256]{2,1,0:T(8,128)(2,1)} %bitcast.36), calls=%async_computation.2 | async-start | bytes 2097152 | tf_op jit(solution)/shard_map/all_to_all | solution.py:93
  92.5 5.7 %copy-start.3 = (bf16[32]{0:T(256)(128)(2,1)S(1)}, bf16[32]{0:T(256)(128)(2,1)}, u32[]{:S(2)}) copy-start(bf16[32]{0:T(256)(128)(2,1)} %param.10) | copy-start | bytes 196
  94.8 29.1 %collective-permute-start = (bf16[2048,256]{1,0:T(8,128)(2,1)}, bf16[2048,256]{1,0:T(8,128)(2,1)}, u32[]{:S(2)}, u32[]{:S(2)}) collective-permute-start(bf16[2048,256]{1,0:T(8,128)(2,1)} %pad_maximum_fusion), channel_id=1, source_target_pairs={{0,64},{64,0},{1,65},{65,1},{2,66},{66,2},{3,67},{67,3},{4,68},{68... | collective-permute-start | bytes 3145736 | tf_op jit(solution)/shard_map/ppermute | solution.py:102
  119.9 12.7 %all-to-all-start.3 = ((f32[8,32,256]{2,1,0:T(8,128)}), f32[8,32,256]{2,1,0:T(8,128)S(1)}, u32[]{:S(2)}, u32[]{:S(2)}) async-start(f32[8,32,256]{2,1,0:T(8,128)} %broadcast_in_dim.46), calls=%async_computation.3 | async-start | bytes 524288 | tf_op jit(solution)/shard_map/all_to_all | solution.py:20
  124.0 16.7 %copy-start.2 = (bf16[32,512]{1,0:T(8,128)(2,1)S(1)}, bf16[32,512]{1,0:T(8,128)(2,1)}, u32[]{:S(2)}) copy-start(bf16[32,512]{1,0:T(8,128)(2,1)} %param.9) | copy-start | bytes 98308
  132.6 8.1 %collective-permute-start.2 = (f32[32,256]{1,0:T(8,128)S(1)}, f32[32,256]{1,0:T(8,128)S(1)}, u32[]{:S(2)}, u32[]{:S(2)}) collective-permute-start(f32[32,256]{1,0:T(8,128)S(1)} %broadcast_multiply_fusion), channel_id=1, source_target_pairs={{0,64},{64,0},{1,65},{65,1},{2,66},{66,2},{3,67},{67,3},{4,68},{68... | collective-permute-start | bytes 98312 | tf_op jit(solution)/shard_map/ppermute | solution.py:96

commit v3 on v1

v3 whole, which is shorter than its diff:
```python
import jax
import jax.numpy as jnp
from jax import lax
from jax.sharding import Mesh
from jax.sharding import PartitionSpec as P

CORE, Z, X, Y = "core", "z", "x", "y"
REPLICA = (Z, CORE)
FSDP = (X, Y)
ALL = (Z, CORE, X, Y)
EPSILON = 1e-06
GROUP = 4
LANES = 128
DIGIT = 64.0


def from_all(value, axes):
    count = lax.axis_size(axes)
    copies = jnp.broadcast_to(value[None], (count, *value.shape))
    return lax.all_to_all(copies, axes, 0, 0, tiled=True)


def to_peer(value, flip):
    count = lax.axis_size(REPLICA)
    return lax.ppermute(value, REPLICA, [(i, i ^ flip) for i in range(count)])


def shards(states, cotangent, kv_weight, norm_gain, prompt_len, response_len, reward_bucket):
    fsdp, replicas = lax.axis_size(FSDP), lax.axis_size(REPLICA)
    member = lax.axis_index(REPLICA)
    place = member % GROUP
    rows_own, features = kv_weight.shape
    quarter = features // GROUP
    seq, width = states.shape[1:]

    def quarter_of(value, flip):
        return lax.dynamic_slice_in_dim(value, (place ^ flip) * quarter, quarter, value.ndim - 1)

    with jax.named_scope("column"):
        reward = reward_bucket.astype(jnp.float32)
        stats = jnp.concatenate([reward, reward * reward, response_len.astype(jnp.float32)])
        stats = from_all(jnp.pad(stats, (0, LANES - 3)), REPLICA)
    others = jnp.arange(replicas)
    rewards = jnp.stack(
        [jnp.sum(jnp.where(others == member ^ flip, stats[:, 0], 0.0)) for flip in range(GROUP)]
    )
    sums = stats.sum(axis=0)
    high = jnp.floor(sums / DIGIT)
    low = sums - DIGIT * high
    extra = jnp.stack([jnp.pad(norm_gain, (0, LANES - rows_own)), high.astype(jnp.bfloat16), low.astype(jnp.bfloat16)])
    with jax.named_scope("weight"):
        filled = from_all(jnp.concatenate([quarter_of(kv_weight, 0), extra]), FSDP)
    weights = [filled[:, :rows_own].reshape(width, quarter)]
    extra = filled[:, rows_own:].astype(jnp.float32)
    gain_own = norm_gain.astype(jnp.float32)
    gain_full = extra[:, 0, :rows_own].reshape(width)
    sums = jnp.sum(DIGIT * extra[:, 1] + extra[:, 2], axis=0)
    count = fsdp * replicas
    average = sums[0] / count
    variance = sums[1] / count - average * average
    grad_scale = lax.rsqrt(variance + EPSILON) * lax.rsqrt(sums[2])

    with jax.named_scope("local"):
        widened = states[0].astype(jnp.float32)
        mean = jnp.mean(widened * widened, axis=-1, keepdims=True)
        unit = widened * lax.rsqrt(mean + EPSILON)
        coarse = lax.reduce_precision(unit, 8, 7)
        fine = (unit - coarse).astype(jnp.bfloat16)
        coarse = coarse.astype(jnp.bfloat16)
        position = jnp.arange(seq, dtype=jnp.int32)
        live = (position >= prompt_len[0]) & (position < prompt_len[0] + response_len[0])
        masked = jnp.where(live[:, None], cotangent[0], jnp.zeros((), cotangent.dtype))

    def product(flip):
        def with_unit(rows):
            part = quarter_of(masked, flip)
            return jnp.einsum("td,tk->dk", rows, part, preferred_element_type=jnp.float32)

        return with_unit(coarse) + with_unit(fine)

    got = {}
    for flip in (3, 2, 1):
        with jax.named_scope(f"peer{flip}"):
            got[flip] = to_peer(product(flip).astype(jnp.bfloat16), flip)
    with jax.named_scope("kept"):
        got[0] = lax.optimization_barrier(product(0))

    scales = rewards - average
    chip = sum(scales[flip] * got[flip].astype(jnp.float32) for flip in range(GROUP))
    chip = chip.astype(jnp.bfloat16).reshape(fsdp, rows_own, quarter)
    with jax.named_scope("plane"):
        plane = lax.all_to_all(chip, FSDP, 0, 0, tiled=True)
    plane = plane.astype(jnp.float32).sum(axis=0)
    with jax.named_scope("last"):
        every = from_all(plane, REPLICA)
    every = every.reshape(replicas // GROUP, GROUP, rows_own, quarter).sum(axis=0)
    total = jnp.concatenate([every[k] for k in range(GROUP)], axis=-1) * grad_scale

    grad_weight = total * (1.0 + gain_own)[:, None]
    grad_gain = jnp.sum(total * kv_weight.astype(jnp.float32), axis=1)

    with jax.named_scope("weight2"):
        weights.append(to_peer(weights[0], 1))
        weights.append(to_peer(weights[0], 2))
    with jax.named_scope("weight3"):
        weights.append(to_peer(weights[2], 1))
    normed = (unit * (1.0 + gain_full)).astype(jnp.bfloat16)
    parts = [
        jnp.dot(normed, w, preferred_element_type=jnp.float32).astype(jnp.bfloat16) for w in weights
    ]
    placed = []
    for k in range(GROUP):
        chosen = parts[0]
        for flip in range(1, GROUP):
            chosen = jnp.where(place ^ flip == k, parts[flip], chosen)
        placed.append(chosen)
    key_values = jnp.concatenate(placed, axis=-1)
    return (key_values[None], grad_weight, grad_gain)


def solution(mesh):
    torus = Mesh(mesh.devices.reshape(8, 2, 8, 8), ALL)
    return jax.shard_map(
        shards,
        mesh=torus,
        in_specs=(
            P(ALL, None, None),
            P(ALL, None, None),
            P(FSDP, None),
            P(FSDP),
            P(ALL),
            P(ALL),
            P(ALL),
        ),
        out_specs=(P(ALL, None, None), P(FSDP, None), P(FSDP)),
        check_vma=False,
    )
```

time: 147 us -> 127 us (0.86)
  the two profiles are of different devices: /device:TPU:4 before, /device:TPU:1 now
where the time goes in v3:
time: 127 us
  starting transfers between devices  66.7 us (53%)
  waiting for transfers between devices  24.9 us (20%)
  other arithmetic  12.5 us (10%)
  matrix products  10.8 us (9%)
  between operations  6.23 us (5%)
  local copies, waits for them, and re-layouts  5.35 us (4%)
    all_to_all x3, starting transfers between devices, from_all(): return lax.all_to_all(copies, axes, 0, 0, tiled=True)  39.7 us
    all_to_all x3, waiting for transfers between devices, from_all(): return lax.all_to_all(copies, axes, 0, 0, tiled=True)  20.6 us
    ppermute x6, starting transfers between devices, to_peer(): return lax.ppermute(value, REPLICA, [(i, i ^ flip) for i in range(count)])  18.6 us
    all_to_all x1, starting transfers between devices, shards(): plane = lax.all_to_all(chip, FSDP, 0, 0, tiled=True)  8.46 us
    dot_general x8, matrix products, with_unit(): jnp.einsum('td,tk->dk', rows, part, preferred_element_type=jnp.float32)  7.47 us
    convert_element_type x1, other arithmetic, shards(): chip = chip.astype(jnp.bfloat16).reshape(fsdp, rows_own, quarter)  4.91 us
    ppermute x6, waiting for transfers between devices, to_peer(): return lax.ppermute(value, REPLICA, [(i, i ^ flip) for i in range(count)])  4.28 us
    dot_general x4, matrix products, shards(): jnp.dot(normed, w, preferred_element_type=jnp.float32).astype(jnp.bfloat16)  3.35 us
  transfers between devices with their start and end apart: 10, of which 3 were waited for; matrix products, arithmetic and copies ran while one was open for 17% of the time, Pallas kernels for 0%

profile of v3, /device:TPU:1, one launch (start us, length us, event | category | flops | bytes accessed | tf_op | source)
XLA Modules:
  0.0 126.5 jit_solution(17882750114823233457)
XLA Ops:
  2.7 18.2 %all-to-all-start = ((f32[16,1,128]{2,1,0:T(1,128)}), f32[16,1,128]{2,1,0:T(1,128)S(1)}, u32[]{:S(2)}, u32[]{:S(2)}) async-start(f32[16,1,128]{2,1,0:T(1,128)} %broadcast_in_dim.44), calls=%async_computation | async-start | bytes 16384 | tf_op jit(solution)/shard_map/column/all_to_all | solution.py:20
  21.5 1.5 %fusion.7 = f32[256]{0:T(256)S(1)} fusion(bf16[1,256,2048]{2,1,0:T(8,128)(2,1)} %param.7), kind=kLoop, calls=%fused_computation.15 | loop fusion | flops 1572608 | bytes 1049600 | tf_op jit(solution)/shard_map/local/reduce_sum | solution.py:65
  23.1 1.1 bitcast_select_fusion
  24.8 1.5 %fusion.5 = bf16[2048,128]{1,0:T(8,128)(2,1)} fusion(f32[2048,128]{1,0:T(8,128)S(1)} %fusion.16, bf16[256,512]{1,0:T(8,128)(2,1)S(1)} %bitcast_select_fusion, s32[]{:T(128)S(6)} %select_n.148, bf16[1,256,2048]{2,1,0:T(8,128)(2,1)S(1)} %copy-done, f32[256]{0:T(256)S(1)} %add_rsqrt_fusion), kind=kOutput, calls=%fused_computation.13 | convolution fusion | flops 137363456 | bytes 2688004 | tf_op jit(solution)/shard_map/peer3/td,tk->dk/dot_general | solution.py:77
  26.3 3.5 %collective-permute-start.5 = (bf16[2048,128]{1,0:T(8,128)(2,1)}, bf16[2048,128]{1,0:T(8,128)(2,1)S(1)}, u32[]{:S(2)}, u32[]{:S(2)}) collective-permute-start(bf16[2048,128]{1,0:T(8,128)(2,1)} %fusion.5), channel_id=1, source_target_pairs={{0,192},{64,128},{128,64},{192,0},{256,448},{320,384},{384,320},{4... | collective-permute-start | bytes 1572872 | tf_op jit(solution)/shard_map/peer3/ppermute | solution.py:25
  30.4 1.4 %fusion.4 = bf16[2048,128]{1,0:T(8,128)(2,1)} fusion(f32[2048,128]{1,0:T(8,128)S(1)} %fusion.19, bf16[256,512]{1,0:T(8,128)(2,1)S(1)} %bitcast_select_fusion, s32[]{:T(128)S(6)} %select_n.147, bf16[1,256,2048]{2,1,0:T(8,128)(2,1)S(1)} %copy-done, f32[256]{0:T(256)S(1)} %add_rsqrt_fusion), kind=kOutput, calls=%fused_computation.12 | convolution fusion | flops 137363456 | bytes 2688004 | tf_op jit(solution)/shard_map/peer2/td,tk->dk/dot_general | solution.py:77
  31.9 1.9 %collective-permute-start.4 = (bf16[2048,128]{1,0:T(8,128)(2,1)}, bf16[2048,128]{1,0:T(8,128)(2,1)}, u32[]{:S(2)}, u32[]{:S(2)}) collective-permute-start(bf16[2048,128]{1,0:T(8,128)(2,1)} %fusion.4), channel_id=1, source_target_pairs={{0,128},{64,192},{128,0},{192,64},{256,384},{320,448},{384,256},{4... | collective-permute-start | bytes 1572872 | tf_op jit(solution)/shard_map/peer2/ppermute | solution.py:25
  34.6 0.9 broadcast_in_dim.45
  35.5 13.2 %all-to-all-start.1 = ((bf16[64,35,128]{2,1,0:T(8,128)(2,1)}), bf16[64,35,128]{2,1,0:T(8,128)(2,1)S(1)}, u32[]{:S(2)}, u32[]{:S(2)}) async-start(bf16[64,35,128]{2,1,0:T(8,128)(2,1)} %broadcast_in_dim.45), calls=%async_computation.1 | async-start | bytes 1310720 | tf_op jit(solution)/shard_map/weight/all_to_all | solution.py:20
  49.3 1.4 %fusion.3 = bf16[2048,128]{1,0:T(8,128)(2,1)} fusion(f32[2048,128]{1,0:T(8,128)S(1)} %fusion.22, bf16[256,512]{1,0:T(8,128)(2,1)S(1)} %bitcast_select_fusion, s32[]{:T(128)S(6)} %select_n.146, bf16[1,256,2048]{2,1,0:T(8,128)(2,1)S(1)} %copy-done, f32[256]{0:T(256)S(1)} %add_rsqrt_fusion), kind=kOutput, calls=%fused_computation.11 | convolution fusion | flops 137363456 | bytes 2688004 | tf_op jit(solution)/shard_map/peer1/td,tk->dk/dot_general | solution.py:77
  50.8 2.7 %collective-permute-start.3 = (bf16[2048,128]{1,0:T(8,128)(2,1)}, bf16[2048,128]{1,0:T(8,128)(2,1)}, u32[]{:S(2)}, u32[]{:S(2)}) collective-permute-start(bf16[2048,128]{1,0:T(8,128)(2,1)} %fusion.3), channel_id=1, source_target_pairs={{0,64},{64,0},{128,192},{192,128},{256,320},{320,256},{384,448},{4... | collective-permute-start | bytes 1572872 | tf_op jit(solution)/shard_map/peer1/ppermute | solution.py:25
  55.5 12.2 %all-to-all-done.1 = bf16[64,35,128]{2,1,0:T(8,128)(2,1)S(1)} async-done(((bf16[64,35,128]{2,1,0:T(8,128)(2,1)}), bf16[64,35,128]{2,1,0:T(8,128)(2,1)S(1)}, u32[]{:S(2)}, u32[]{:S(2)}) %all-to-all-start.1) | async-done | bytes 573472 | tf_op jit(solution)/shard_map/weight/all_to_all | solution.py:20
  69.0 2.6 %maximum_subtract_fusion = f32[4]{0:T(128)S(1)} fusion(f32[1]{0:T(128)} %bitcast.10, f32[1]{0:T(128)} %bitcast.9, f32[1]{0:T(128)} %bitcast.8, f32[1]{0:T(128)} %bitcast.7, f32[]{:T(128)} %bitcast.11), kind=kLoop, calls=%fused_computation.83 | loop fusion | flops 16 | bytes 36 | tf_op jit(solution)/shard_map/sub | solution.py:88
  72.3 4.9 %add_convert_fusion = bf16[2048,128]{1,0:T(8,128)(2,1)} fusion(bf16[2048,128]{1,0:T(8,128)(2,1)S(1)} %collective-permute-done.5, bf16[2048,128]{1,0:T(8,128)(2,1)} %collective-permute-done.4, bf16[2048,128]{1,0:T(8,128)(2,1)} %collective-permute-done.3, f32[2048,128]{1,0:T(8,128)S(1)} %convolution_add_fusion.3, f32[]{:T(128)} %bitcast.18, f32[]{:T(128)} %bitcast.17, ...), kind=kLoop, calls=%fused_computation.25 | loop fusion | flops 2883584 | bytes 3145744 | tf_op jit(solution)/shard_map/convert_element_type | solution.py:90
  77.2 8.5 %all-to-all-start.2 = ((bf16[64,32,128]{2,1,0:T(8,128)(2,1)}), bf16[64,32,128]{2,1,0:T(8,128)(2,1)S(1)}, u32[]{:S(2)}, u32[]{:S(2)}) async-start(bf16[64,32,128]{2,1,0:T(8,128)(2,1)} %bitcast.19), calls=%async_computation.2 | async-start | bytes 1048576 | tf_op jit(solution)/shard_map/plane/all_to_all | solution.py:92
  85.7 3.4 %collective-permute-start = (bf16[2048,128]{1,0:T(8,128)(2,1)S(1)}, bf16[2048,128]{1,0:T(8,128)(2,1)S(1)}, u32[]{:S(2)}, u32[]{:S(2)}) collective-permute-start(bf16[2048,128]{1,0:T(8,128)(2,1)S(1)} %bitcast.83), channel_id=1, source_target_pairs={{0,128},{64,192},{128,0},{192,64},{256,384},{320,448},{384,256},{4... | collective-permute-start | bytes 1572872 | tf_op jit(solution)/shard_map/weight2/ppermute | solution.py:25
  89.1 3.3 %collective-permute-start.2 = (bf16[2048,128]{1,0:T(8,128)(2,1)S(1)}, bf16[2048,128]{1,0:T(8,128)(2,1)S(1)}, u32[]{:S(2)}, u32[]{:S(2)}) collective-permute-start(bf16[2048,128]{1,0:T(8,128)(2,1)S(1)} %bitcast.84), channel_id=1, source_target_pairs={{0,64},{64,0},{128,192},{192,128},{256,320},{320,256},{384,448},{4... | collective-permute-start | bytes 1572872 | tf_op jit(solution)/shard_map/weight2/ppermute | solution.py:25
  95.8 4.3 %collective-permute-done = bf16[2048,128]{1,0:T(8,128)(2,1)S(1)} collective-permute-done((bf16[2048,128]{1,0:T(8,128)(2,1)S(1)}, bf16[2048,128]{1,0:T(8,128)(2,1)S(1)}, u32[]{:S(2)}, u32[]{:S(2)}) %collective-permute-start) | collective-permute-done | bytes 524320 | tf_op jit(solution)/shard_map/weight2/ppermute | solution.py:25
  100.0 3.8 %collective-permute-start.1 = (bf16[2048,128]{1,0:T(8,128)(2,1)S(1)}, bf16[2048,128]{1,0:T(8,128)(2,1)}, u32[]{:S(2)}, u32[]{:S(2)}) collective-permute-start(bf16[2048,128]{1,0:T(8,128)(2,1)S(1)} %collective-permute-done), channel_id=1, source_target_pairs={{0,64},{64,0},{128,192},{192,128},{256,320},{320,256},{384,448},{4... | collective-permute-start | bytes 1572872 | tf_op jit(solution)/shard_map/weight3/ppermute | solution.py:25
  105.3 8.3 %all-to-all-start.3 = ((f32[16,32,128]{2,1,0:T(8,128)}), f32[16,32,128]{2,1,0:T(8,128)S(1)}, u32[]{:S(2)}, u32[]{:S(2)}) async-start(f32[16,32,128]{2,1,0:T(8,128)} %broadcast_in_dim.50), calls=%async_computation.3 | async-start | bytes 524288 | tf_op jit(solution)/shard_map/last/all_to_all | solution.py:20
  114.2 1.6 %select_select_fusion.3 = (bf16[256,128]{0,1:T(8,128)(2,1)S(1)}, bf16[256,128]{0,1:T(8,128)(2,1)S(1)}, bf16[256,128]{0,1:T(8,128)(2,1)S(1)}, bf16[256,128]{0,1:T(8,128)(2,1)S(1)}) fusion(bf16[256,128]{0,1:T(8,128)(2,1)S(1)} %convolution_convert_fusion.2, bf16[256,128]{0,1:T(8,128)(2,1)S(1)} %convolution_convert_fusion.1, ...), kind=kOutput, calls=%fused_computation.36 | convolution fusion | flops 136740864 | bytes 2040844 | tf_op jit(solution)/shard_map/dot_general | solution.py:109
  115.8 0.8 copy.15
  116.7 8.5 %all-to-all-done.3 = f32[16,32,128]{2,1,0:T(8,128)S(1)} async-done(((f32[16,32,128]{2,1,0:T(8,128)}), f32[16,32,128]{2,1,0:T(8,128)S(1)}, u32[]{:S(2)}, u32[]{:S(2)}) %all-to-all-start.3) | async-done | bytes 262176 | tf_op jit(solution)/shard_map/last/all_to_all | solution.py:20
  125.2 1.3 %multiply_reduce_fusion = (f32[32]{0:T(128)}, f32[32,512]{1,0:T(8,128)}) fusion(bf16[32,512]{1,0:T(8,128)(2,1)S(1)} %copy-done.1, f32[32,128]{1,0:T(8,128)S(1)} %get-tuple-element.32, f32[32,128]{1,0:T(8,128)S(1)} %get-tuple-element.33, f32[32,128]{1,0:T(8,128)S(1)} %get-tuple-element.34, f32[32,128]{1,0:T(8,128)S(1)} %get-tuple-element.31, f32[]{:T(128)} %bitcast.25, ...), kind=kLoop, calls=%fused_computation.32 | loop fusion | flops 131040 | bytes 164100 | tf_op jit(solution)/shard_map/reduce_sum | solution.py:100
  (45 shorter events, 9.6 us)
Async XLA Ops:
  0.6 23.5 %copy-start = (bf16[1,256,2048]{2,1,0:T(8,128)(2,1)S(1)}, bf16[1,256,2048]{2,1,0:T(8,128)(2,1)}, u32[]{:S(2)}) copy-start(bf16[1,256,2048]{2,1,0:T(8,128)(2,1)} %param.7) | copy-start | bytes 3145732
  2.7 31.8 %all-to-all-start = ((f32[16,1,128]{2,1,0:T(1,128)}), f32[16,1,128]{2,1,0:T(1,128)S(1)}, u32[]{:S(2)}, u32[]{:S(2)}) async-start(f32[16,1,128]{2,1,0:T(1,128)} %broadcast_in_dim.44), calls=%async_computation | async-start | bytes 16384 | tf_op jit(solution)/shard_map/column/all_to_all | solution.py:20
  26.3 46.0 %collective-permute-start.5 = (bf16[2048,128]{1,0:T(8,128)(2,1)}, bf16[2048,128]{1,0:T(8,128)(2,1)S(1)}, u32[]{:S(2)}, u32[]{:S(2)}) collective-permute-start(bf16[2048,128]{1,0:T(8,128)(2,1)} %fusion.5), channel_id=1, source_target_pairs={{0,192},{64,128},{128,64},{192,0},{256,448},{320,384},{384,320},{4... | collective-permute-start | bytes 1572872 | tf_op jit(solution)/shard_map/peer3/ppermute | solution.py:25
  30.4 4.1 %copy-start.2 = (bf16[32]{0:T(256)(128)(2,1)S(1)}, bf16[32]{0:T(256)(128)(2,1)}, u32[]{:S(2)}) copy-start(bf16[32]{0:T(256)(128)(2,1)} %param.10) | copy-start | bytes 196
  31.9 40.4 %collective-permute-start.4 = (bf16[2048,128]{1,0:T(8,128)(2,1)}, bf16[2048,128]{1,0:T(8,128)(2,1)}, u32[]{:S(2)}, u32[]{:S(2)}) collective-permute-start(bf16[2048,128]{1,0:T(8,128)(2,1)} %fusion.4), channel_id=1, source_target_pairs={{0,128},{64,192},{128,0},{192,64},{256,384},{320,448},{384,256},{4... | collective-permute-start | bytes 1572872 | tf_op jit(solution)/shard_map/peer2/ppermute | solution.py:25
  35.5 32.1 %all-to-all-start.1 = ((bf16[64,35,128]{2,1,0:T(8,128)(2,1)}), bf16[64,35,128]{2,1,0:T(8,128)(2,1)S(1)}, u32[]{:S(2)}, u32[]{:S(2)}) async-start(bf16[64,35,128]{2,1,0:T(8,128)(2,1)} %broadcast_in_dim.45), calls=%async_computation.1 | async-start | bytes 1310720 | tf_op jit(solution)/shard_map/weight/all_to_all | solution.py:20
  50.8 21.5 %collective-permute-start.3 = (bf16[2048,128]{1,0:T(8,128)(2,1)}, bf16[2048,128]{1,0:T(8,128)(2,1)}, u32[]{:S(2)}, u32[]{:S(2)}) collective-permute-start(bf16[2048,128]{1,0:T(8,128)(2,1)} %fusion.3), channel_id=1, source_target_pairs={{0,64},{64,0},{128,192},{192,128},{256,320},{320,256},{384,448},{4... | collective-permute-start | bytes 1572872 | tf_op jit(solution)/shard_map/peer1/ppermute | solution.py:25
  77.2 27.3 %all-to-all-start.2 = ((bf16[64,32,128]{2,1,0:T(8,128)(2,1)}), bf16[64,32,128]{2,1,0:T(8,128)(2,1)S(1)}, u32[]{:S(2)}, u32[]{:S(2)}) async-start(bf16[64,32,128]{2,1,0:T(8,128)(2,1)} %bitcast.19), calls=%async_computation.2 | async-start | bytes 1048576 | tf_op jit(solution)/shard_map/plane/all_to_all | solution.py:92
  85.7 14.3 %collective-permute-start = (bf16[2048,128]{1,0:T(8,128)(2,1)S(1)}, bf16[2048,128]{1,0:T(8,128)(2,1)S(1)}, u32[]{:S(2)}, u32[]{:S(2)}) collective-permute-start(bf16[2048,128]{1,0:T(8,128)(2,1)S(1)} %bitcast.83), channel_id=1, source_target_pairs={{0,128},{64,192},{128,0},{192,64},{256,384},{320,448},{384,256},{4... | collective-permute-start | bytes 1572872 | tf_op jit(solution)/shard_map/weight2/ppermute | solution.py:25
  89.1 24.5 %collective-permute-start.2 = (bf16[2048,128]{1,0:T(8,128)(2,1)S(1)}, bf16[2048,128]{1,0:T(8,128)(2,1)S(1)}, u32[]{:S(2)}, u32[]{:S(2)}) collective-permute-start(bf16[2048,128]{1,0:T(8,128)(2,1)S(1)} %bitcast.84), channel_id=1, source_target_pairs={{0,64},{64,0},{128,192},{192,128},{256,320},{320,256},{384,448},{4... | collective-permute-start | bytes 1572872 | tf_op jit(solution)/shard_map/weight2/ppermute | solution.py:25
  100.0 14.1 %collective-permute-start.1 = (bf16[2048,128]{1,0:T(8,128)(2,1)S(1)}, bf16[2048,128]{1,0:T(8,128)(2,1)}, u32[]{:S(2)}, u32[]{:S(2)}) collective-permute-start(bf16[2048,128]{1,0:T(8,128)(2,1)S(1)} %collective-permute-done), channel_id=1, source_target_pairs={{0,64},{64,0},{128,192},{192,128},{256,320},{320,256},{384,448},{4... | collective-permute-start | bytes 1572872 | tf_op jit(solution)/shard_map/weight3/ppermute | solution.py:25
  105.3 19.9 %all-to-all-start.3 = ((f32[16,32,128]{2,1,0:T(8,128)}), f32[16,32,128]{2,1,0:T(8,128)S(1)}, u32[]{:S(2)}, u32[]{:S(2)}) async-start(f32[16,32,128]{2,1,0:T(8,128)} %broadcast_in_dim.50), calls=%async_computation.3 | async-start | bytes 524288 | tf_op jit(solution)/shard_map/last/all_to_all | solution.py:20
  115.8 9.4 %copy-start.1 = (bf16[32,512]{1,0:T(8,128)(2,1)S(1)}, bf16[32,512]{1,0:T(8,128)(2,1)}, u32[]{:S(2)}) copy-start(bf16[32,512]{1,0:T(8,128)(2,1)} %param.9) | copy-start | bytes 98308

commit v4 on v3

v4 whole, which is shorter than its diff:
```python
import functools

import jax
import jax.numpy as jnp
from jax import lax
from jax.experimental import pallas as pl
from jax.experimental.pallas import tpu as pltpu
from jax.sharding import Mesh
from jax.sharding import PartitionSpec as P

CORE, Z, X, Y = "core", "z", "x", "y"
REPLICA = (Z, CORE)
FSDP = (X, Y)
ALL = (Z, CORE, X, Y)
EPSILON = 1e-06
GROUP = 4
LANES = 128
DIGIT = 64.0
STEP = 128


def from_all(value, axes):
    count = lax.axis_size(axes)
    copies = jnp.broadcast_to(value[None], (count, *value.shape))
    return lax.all_to_all(copies, axes, 0, 0, tiled=True)


def to_peer(value, flip):
    count = lax.axis_size(REPLICA)
    return lax.ppermute(value, REPLICA, [(i, i ^ flip) for i in range(count)])


def combine(count, rewards_ref, filled_ref, kept_ref, *refs):
    *got_refs, out_ref = refs
    width, _ = out_ref.shape
    extra_rows = filled_ref.shape[1] - 3
    digits = filled_ref[:, extra_rows:, :].astype(jnp.float32).sum(axis=0)
    sums = DIGIT * digits[1:2] + digits[2:3]
    average = sums[0, 0] / count
    scales = [rewards_ref[flip] - average for flip in range(GROUP)]

    def block(step, carry):
        rows = pl.ds(step * STEP, STEP)
        chip = scales[0] * kept_ref[rows, :]
        for flip in range(1, GROUP):
            chip += scales[flip] * got_refs[flip - 1][rows, :].astype(jnp.float32)
        out_ref[rows, :] = chip.astype(out_ref.dtype)
        return carry

    lax.fori_loop(0, width // STEP, block, 0)


def combined(rewards, filled, parts, count):
    width, quarter = parts[0].shape
    vmem = pl.BlockSpec(memory_space=pltpu.VMEM)
    return pl.pallas_call(
        functools.partial(combine, count),
        out_shape=jax.ShapeDtypeStruct((width, quarter), jnp.bfloat16),
        in_specs=[pl.BlockSpec(memory_space=pltpu.SMEM), *([vmem] * (1 + GROUP))],
        out_specs=vmem,
        compiler_params=pltpu.CompilerParams(vmem_limit_bytes=16 * 2**20),
        cost_estimate=pl.CostEstimate(
            flops=8 * width * quarter, bytes_accessed=12 * width * quarter, transcendentals=0
        ),
        name="combine",
    )(rewards, filled, *parts)


def shards(states, cotangent, kv_weight, norm_gain, prompt_len, response_len, reward_bucket):
    fsdp, replicas = lax.axis_size(FSDP), lax.axis_size(REPLICA)
    member = lax.axis_index(REPLICA)
    place = member % GROUP
    rows_own, features = kv_weight.shape
    quarter = features // GROUP
    seq, width = states.shape[1:]

    def quarter_of(value, flip):
        return lax.dynamic_slice_in_dim(value, (place ^ flip) * quarter, quarter, value.ndim - 1)

    reward = reward_bucket.astype(jnp.float32)
    stats = jnp.concatenate([reward, reward * reward, response_len.astype(jnp.float32)])
    stats = from_all(jnp.pad(stats, (0, LANES - 3)), REPLICA)
    others = jnp.arange(replicas)
    rewards = jnp.stack(
        [jnp.sum(jnp.where(others == member ^ flip, stats[:, 0], 0.0)) for flip in range(GROUP)]
    )
    sums = stats.sum(axis=0)
    high = jnp.floor(sums / DIGIT)
    low = sums - DIGIT * high
    extra = jnp.stack([jnp.pad(norm_gain, (0, LANES - rows_own)), high.astype(jnp.bfloat16), low.astype(jnp.bfloat16)])
    filled = from_all(jnp.concatenate([quarter_of(kv_weight, 0), extra]), FSDP)
    weights = [filled[:, :rows_own].reshape(width, quarter)]
    extra = filled[:, rows_own:].astype(jnp.float32)
    gain_own = norm_gain.astype(jnp.float32)
    gain_full = extra[:, 0, :rows_own].reshape(width)
    sums = jnp.sum(DIGIT * extra[:, 1] + extra[:, 2], axis=0)
    count = fsdp * replicas
    average = sums[0] / count
    variance = sums[1] / count - average * average
    grad_scale = lax.rsqrt(variance + EPSILON) * lax.rsqrt(sums[2])

    widened = states[0].astype(jnp.float32)
    mean = jnp.mean(widened * widened, axis=-1, keepdims=True)
    unit = widened * lax.rsqrt(mean + EPSILON)
    coarse = lax.reduce_precision(unit, 8, 7)
    fine = (unit - coarse).astype(jnp.bfloat16)
    coarse = coarse.astype(jnp.bfloat16)
    position = jnp.arange(seq, dtype=jnp.int32)
    live = (position >= prompt_len[0]) & (position < prompt_len[0] + response_len[0])
    masked = jnp.where(live[:, None], cotangent[0], jnp.zeros((), cotangent.dtype))

    def product(flip):
        def with_unit(rows):
            part = quarter_of(masked, flip)
            return jnp.einsum("td,tk->dk", rows, part, preferred_element_type=jnp.float32)

        return with_unit(coarse) + with_unit(fine)

    got = {}
    for flip in (3, 2, 1):
        got[flip] = to_peer(product(flip).astype(jnp.bfloat16), flip)
    got[0] = lax.optimization_barrier(product(0))

    chip = combined(rewards, filled, [got[flip] for flip in range(GROUP)], count)
    chip = chip.reshape(fsdp, rows_own, quarter)
    plane = lax.all_to_all(chip, FSDP, 0, 0, tiled=True)
    plane = plane.astype(jnp.float32).sum(axis=0)
    every = from_all(plane, REPLICA)
    every = every.reshape(replicas // GROUP, GROUP, rows_own, quarter).sum(axis=0)
    total = jnp.concatenate([every[k] for k in range(GROUP)], axis=-1) * grad_scale

    grad_weight = total * (1.0 + gain_own)[:, None]
    grad_gain = jnp.sum(total * kv_weight.astype(jnp.float32), axis=1)

    weights.append(to_peer(weights[0], 1))
    weights.append(to_peer(weights[0], 2))
    weights.append(to_peer(weights[2], 1))
    normed = (unit * (1.0 + gain_full)).astype(jnp.bfloat16)
    parts = [
        jnp.dot(normed, w, preferred_element_type=jnp.float32).astype(jnp.bfloat16) for w in weights
    ]
    placed = []
    for k in range(GROUP):
        chosen = parts[0]
        for flip in range(1, GROUP):
            chosen = jnp.where(place ^ flip == k, parts[flip], chosen)
        placed.append(chosen)
    key_values = jnp.concatenate(placed, axis=-1)
    return (key_values[None], grad_weight, grad_gain)


def solution(mesh):
    torus = Mesh(mesh.devices.reshape(8, 2, 8, 8), ALL)

    return jax.shard_map(
        shards,
        mesh=torus,
        in_specs=(
            P(ALL, None, None),
            P(ALL, None, None),
            P(FSDP, None),
            P(FSDP),
            P(ALL),
            P(ALL),
            P(ALL),
        ),
        out_specs=(P(ALL, None, None), P(FSDP, None), P(FSDP)),
        check_vma=False,
    )
```

time: 127 us -> 143 us (1.13)
  waiting for transfers between devices: 24.9 us -> 45 us
  other arithmetic: 12.5 us -> 7.73 us
  starting transfers between devices: 66.7 us -> 62.7 us
  matrix products: 10.8 us -> 12.9 us
  Pallas kernels: 0 us -> 1.9 us
    all_to_all x3, waiting for transfers between devices: 20.6 us -> 37.3 us  [from_all(): return lax.all_to_all(copies, axes, 0, 0, tiled=True)]
    all_to_all x3, starting transfers between devices: 39.7 us -> 24.1 us  [from_all(): return lax.all_to_all(copies, axes, 0, 0, tiled=True)]
    ppermute x6, starting transfers between devices: 18.6 us -> 32.5 us  [to_peer(): return lax.ppermute(value, REPLICA, [(i, i ^ flip) for i in range(count)])]
    all_to_all x1, waiting for transfers between devices: 0.01 us -> 7.63 us  [shards(): plane = lax.all_to_all(chip, FSDP, 0, 0, tiled=True)]
    convert_element_type x1 -> x0, other arithmetic: 4.91 us -> none  [shards(): chip = chip.astype(jnp.bfloat16).reshape(fsdp, rows_own, quarter)]
    ppermute x6, waiting for transfers between devices: 4.28 us -> 0.02 us  [to_peer(): return lax.ppermute(value, REPLICA, [(i, i ^ flip) for i in range(count)])]
    another operation x0 -> x1, other arithmetic: none -> 2.63 us  [shards(): jnp.stack([jnp.sum(jnp.where(others == member ^ flip, stats[:, 0], 0.0))...]
    sub x1 -> x0, other arithmetic: 2.58 us -> none  [shards(): scales = rewards - average]
  transfers between devices with their start and end apart: 10 -> 10, of which waited for: 3 -> 4; matrix products, arithmetic and copies ran while one was open for 17% -> 14% of each run, Pallas kernels for 0% -> 1%
where the time goes in v4:
time: 143 us; the launch traced here: 142 us
  starting transfers between devices  62.7 us (44%)
  waiting for transfers between devices  45 us (31%)
  matrix products  12.9 us (9%)
  other arithmetic  7.73 us (5%)
  local copies, waits for them, and re-layouts  6.02 us (4%)
  between operations  5.58 us (4%)
  Pallas kernels  1.9 us (1%)
    all_to_all x3, waiting for transfers between devices, from_all(): return lax.all_to_all(copies, axes, 0, 0, tiled=True)  37.3 us
    ppermute x6, starting transfers between devices, to_peer(): return lax.ppermute(value, REPLICA, [(i, i ^ flip) for i in range(count)])  32.5 us
    all_to_all x3, starting transfers between devices, from_all(): return lax.all_to_all(copies, axes, 0, 0, tiled=True)  24.1 us
    all_to_all x1, waiting for transfers between devices, shards(): plane = lax.all_to_all(chip, FSDP, 0, 0, tiled=True)  7.63 us
    dot_general x8, matrix products, with_unit(): jnp.einsum('td,tk->dk', rows, part, preferred_element_type=jnp.float32)  7.47 us
    all_to_all x1, starting transfers between devices, shards(): plane = lax.all_to_all(chip, FSDP, 0, 0, tiled=True)  6.11 us
    dot_general x4, matrix products, shards(): jnp.dot(normed, w, preferred_element_type=jnp.float32).astype(jnp.bfloat16)  5.44 us
  transfers between devices with their start and end apart: 10, of which 4 were waited for; matrix products, arithmetic and copies ran while one was open for 14% of the time, Pallas kernels for 1%

profile of v4, /device:TPU:1, one launch (start us, length us, event | category | flops | bytes accessed | tf_op | source)
XLA Modules:
  0.0 141.8 jit_solution(17635047335480218074)
XLA Ops:
  0.7 1.6 %fusion.7 = f32[256]{0:T(256)S(1)} fusion(bf16[1,256,2048]{2,1,0:T(8,128)(2,1)} %param.7), kind=kLoop, calls=%fused_computation.15 | loop fusion | flops 1572608 | bytes 1049600 | tf_op jit(solution)/shard_map/reduce_sum | solution.py:103
  5.3 1.4 %fusion.3 = bf16[2048,128]{1,0:T(8,128)(2,1)} fusion(f32[2048,128]{1,0:T(8,128)S(1)} %fusion.22, bf16[256,512]{1,0:T(8,128)(2,1)S(1)} %bitcast_select_fusion, s32[]{:T(128)S(6)} %select_n.146, bf16[1,256,2048]{2,1,0:T(8,128)(2,1)S(1)} %copy-done, f32[256]{0:T(256)S(1)} %add_rsqrt_fusion), kind=kOutput, calls=%fused_computation.11 | convolution fusion | flops 137363456 | bytes 2688004 | tf_op jit(solution)/shard_map/td,tk->dk/dot_general | solution.py:115
  6.7 16.0 %collective-permute-start.3 = (bf16[2048,128]{1,0:T(8,128)(2,1)}, bf16[2048,128]{1,0:T(8,128)(2,1)S(1)}, u32[]{:S(2)}, u32[]{:S(2)}) collective-permute-start(bf16[2048,128]{1,0:T(8,128)(2,1)} %fusion.3), channel_id=1, source_target_pairs={{0,64},{64,0},{128,192},{192,128},{256,320},{320,256},{384,448},{4... | collective-permute-start | bytes 1572872 | tf_op jit(solution)/shard_map/ppermute | solution.py:30
  23.4 1.4 %fusion.4 = bf16[2048,128]{1,0:T(8,128)(2,1)} fusion(f32[2048,128]{1,0:T(8,128)S(1)} %fusion.19, bf16[256,512]{1,0:T(8,128)(2,1)S(1)} %bitcast_select_fusion, s32[]{:T(128)S(6)} %select_n.147, bf16[1,256,2048]{2,1,0:T(8,128)(2,1)S(1)} %copy-done, f32[256]{0:T(256)S(1)} %add_rsqrt_fusion), kind=kOutput, calls=%fused_computation.12 | convolution fusion | flops 137363456 | bytes 2688004 | tf_op jit(solution)/shard_map/td,tk->dk/dot_general | solution.py:115
  24.8 1.9 %collective-permute-start.4 = (bf16[2048,128]{1,0:T(8,128)(2,1)}, bf16[2048,128]{1,0:T(8,128)(2,1)S(1)}, u32[]{:S(2)}, u32[]{:S(2)}) collective-permute-start(bf16[2048,128]{1,0:T(8,128)(2,1)} %fusion.4), channel_id=1, source_target_pairs={{0,128},{64,192},{128,0},{192,64},{256,384},{320,448},{384,256},{4... | collective-permute-start | bytes 1572872 | tf_op jit(solution)/shard_map/ppermute | solution.py:30
  27.4 1.4 %fusion.5 = bf16[2048,128]{1,0:T(8,128)(2,1)} fusion(f32[2048,128]{1,0:T(8,128)S(1)} %fusion.16, bf16[256,512]{1,0:T(8,128)(2,1)S(1)} %bitcast_select_fusion, s32[]{:T(128)S(6)} %select_n.148, bf16[1,256,2048]{2,1,0:T(8,128)(2,1)S(1)} %copy-done, f32[256]{0:T(256)S(1)} %add_rsqrt_fusion), kind=kOutput, calls=%fused_computation.13 | convolution fusion | flops 137363456 | bytes 2688004 | tf_op jit(solution)/shard_map/td,tk->dk/dot_general | solution.py:115
  28.9 3.5 %collective-permute-start.5 = (bf16[2048,128]{1,0:T(8,128)(2,1)}, bf16[2048,128]{1,0:T(8,128)(2,1)S(1)}, u32[]{:S(2)}, u32[]{:S(2)}) collective-permute-start(bf16[2048,128]{1,0:T(8,128)(2,1)} %fusion.5), channel_id=1, source_target_pairs={{0,192},{64,128},{128,64},{192,0},{256,448},{320,384},{384,320},{4... | collective-permute-start | bytes 1572872 | tf_op jit(solution)/shard_map/ppermute | solution.py:30
  33.7 4.3 %all-to-all-start = ((f32[16,1,128]{2,1,0:T(1,128)}), f32[16,1,128]{2,1,0:T(1,128)S(1)}, u32[]{:S(2)}, u32[]{:S(2)}) async-start(f32[16,1,128]{2,1,0:T(1,128)} %broadcast_in_dim.44), calls=%async_computation | async-start | bytes 16384 | tf_op jit(solution)/shard_map/all_to_all | solution.py:25
  38.7 15.5 %all-to-all-done = f32[16,1,128]{2,1,0:T(1,128)S(1)} async-done(((f32[16,1,128]{2,1,0:T(1,128)}), f32[16,1,128]{2,1,0:T(1,128)S(1)}, u32[]{:S(2)}, u32[]{:S(2)}) %all-to-all-start) | async-done | bytes 8224 | tf_op jit(solution)/shard_map/all_to_all | solution.py:25
  55.2 13.2 %all-to-all-start.1 = ((bf16[64,35,128]{2,1,0:T(8,128)(2,1)}), bf16[64,35,128]{2,1,0:T(8,128)(2,1)S(1)}, u32[]{:S(2)}, u32[]{:S(2)}) async-start(bf16[64,35,128]{2,1,0:T(8,128)(2,1)} %broadcast_in_dim.45), calls=%async_computation.1 | async-start | bytes 1310720 | tf_op jit(solution)/shard_map/all_to_all | solution.py:25
  71.0 2.6 %pad_maximum_fusion.1.rewards_ref = f32[4]{0:T(128)S(1)} fusion(f32[1]{0:T(128)} %bitcast.10, f32[1]{0:T(128)} %bitcast.9, f32[1]{0:T(128)} %bitcast.8, f32[1]{0:T(128)} %bitcast.7), kind=kLoop, calls=%fused_computation.82 | loop fusion | flops 12 | bytes 32 | tf_op jit(solution)/shard_map/stack | solution.py:84
  73.6 13.4 %all-to-all-done.1.filled_ref = bf16[64,35,128]{2,1,0:T(8,128)(2,1)S(1)} async-done(((bf16[64,35,128]{2,1,0:T(8,128)(2,1)}), bf16[64,35,128]{2,1,0:T(8,128)(2,1)S(1)}, u32[]{:S(2)}, u32[]{:S(2)}) %all-to-all-start.1) | async-done | bytes 573472 | tf_op jit(solution)/shard_map/all_to_all | solution.py:25
  87.8 5.4 %collective-permute-start.2 = (bf16[2048,128]{1,0:T(8,128)(2,1)}, bf16[2048,128]{1,0:T(8,128)(2,1)}, u32[]{:S(2)}, u32[]{:S(2)}) collective-permute-start(bf16[2048,128]{1,0:T(8,128)(2,1)} %bitcast.3), channel_id=1, source_target_pairs={{0,64},{64,0},{128,192},{192,128},{256,320},{320,256},{384,448},{4... | collective-permute-start | bytes 1572872 | tf_op jit(solution)/shard_map/ppermute | solution.py:30
  93.3 3.1 %collective-permute-start = (bf16[2048,128]{1,0:T(8,128)(2,1)}, bf16[2048,128]{1,0:T(8,128)(2,1)}, u32[]{:S(2)}, u32[]{:S(2)}) collective-permute-start(bf16[2048,128]{1,0:T(8,128)(2,1)} %bitcast.3), channel_id=1, source_target_pairs={{0,128},{64,192},{128,0},{192,64},{256,384},{320,448},{384,256},{4... | collective-permute-start | bytes 1572872 | tf_op jit(solution)/shard_map/ppermute | solution.py:30
  96.4 1.9 %combine.1 = bf16[2048,128]{1,0:T(8,128)(2,1)} custom-call(f32[4]{0:T(128)S(1)} %pad_maximum_fusion.1.rewards_ref, bf16[64,35,128]{2,1,0:T(8,128)(2,1)S(1)} %all-to-all-done.1.filled_ref, f32[2048,128]{1,0:T(8,128)S(1)} %convolution_add_fusion.3.kept_ref, bf16[2048,128]{1,0:T(8,128)(2,1)S(1)} %collective-permute-done.3.refs_0_, ...), custom_call_target="tpu_custom_call" | custom-call | flops 2097152 | bytes 3145728 | tf_op jit(solution)/shard_map/combine/pallas_call | solution.py:56
  98.3 6.1 %all-to-all-start.2 = ((bf16[64,32,128]{2,1,0:T(8,128)(2,1)}), bf16[64,32,128]{2,1,0:T(8,128)(2,1)S(1)}, u32[]{:S(2)}, u32[]{:S(2)}) async-start(bf16[64,32,128]{2,1,0:T(8,128)(2,1)} %bitcast.14), calls=%async_computation.2 | async-start | bytes 1048576 | tf_op jit(solution)/shard_map/all_to_all | solution.py:126
  104.6 1.6 %convolution_convert_fusion = bf16[256,128]{0,1:T(8,128)(2,1)S(1)} fusion(bf16[2048,128]{1,0:T(8,128)(2,1)} %bitcast.3, bf16[1,256,2048]{2,1,0:T(8,128)(2,1)S(1)} %copy-done.2, f32[2048]{0:T(1024)S(1)} %add.90, f32[256]{0:T(256)S(1)} %add_rsqrt_fusion), kind=kOutput, calls=%fused_computation.19 | convolution fusion | flops 136347648 | bytes 1647616 | tf_op jit(solution)/shard_map/dot_general | solution.py:140
  109.6 2.5 %collective-permute-start.1 = (bf16[2048,128]{1,0:T(8,128)(2,1)}, bf16[2048,128]{1,0:T(8,128)(2,1)S(1)}, u32[]{:S(2)}, u32[]{:S(2)}) collective-permute-start(bf16[2048,128]{1,0:T(8,128)(2,1)} %collective-permute-done), channel_id=1, source_target_pairs={{0,64},{64,0},{128,192},{192,128},{256,320},{320,256},{384,448},{4... | collective-permute-start | bytes 1572872 | tf_op jit(solution)/shard_map/ppermute | solution.py:30
  112.1 1.6 %convolution_convert_fusion.2 = bf16[256,128]{0,1:T(8,128)(2,1)S(1)} fusion(bf16[2048,128]{1,0:T(8,128)(2,1)} %collective-permute-done, bf16[1,256,2048]{2,1,0:T(8,128)(2,1)S(1)} %copy-done.2, f32[2048]{0:T(1024)S(1)} %add.90, f32[256]{0:T(256)S(1)} %add_rsqrt_fusion), kind=kOutput, calls=%fused_computation.21 | convolution fusion | flops 136347648 | bytes 1647616 | tf_op jit(solution)/shard_map/dot_general | solution.py:140
  113.7 7.6 %all-to-all-done.2 = bf16[64,32,128]{2,1,0:T(8,128)(2,1)S(1)} async-done(((bf16[64,32,128]{2,1,0:T(8,128)(2,1)}), bf16[64,32,128]{2,1,0:T(8,128)(2,1)S(1)}, u32[]{:S(2)}, u32[]{:S(2)}) %all-to-all-start.2) | async-done | bytes 524320 | tf_op jit(solution)/shard_map/all_to_all | solution.py:126
  122.2 6.6 %all-to-all-start.3 = ((f32[16,32,128]{2,1,0:T(8,128)}), f32[16,32,128]{2,1,0:T(8,128)S(1)}, u32[]{:S(2)}, u32[]{:S(2)}) async-start(f32[16,32,128]{2,1,0:T(8,128)} %broadcast_in_dim.50), calls=%async_computation.3 | async-start | bytes 524288 | tf_op jit(solution)/shard_map/all_to_all | solution.py:25
  128.8 1.6 %convolution_convert_fusion.1 = bf16[256,128]{0,1:T(8,128)(2,1)S(1)} fusion(bf16[2048,128]{1,0:T(8,128)(2,1)} %collective-permute-done.2, bf16[1,256,2048]{2,1,0:T(8,128)(2,1)S(1)} %copy-done.2, f32[2048]{0:T(1024)S(1)} %add.90, f32[256]{0:T(256)S(1)} %add_rsqrt_fusion), kind=kOutput, calls=%fused_computation.20 | convolution fusion | flops 136347648 | bytes 1647616 | tf_op jit(solution)/shard_map/dot_general | solution.py:140
  131.9 8.5 %all-to-all-done.3 = f32[16,32,128]{2,1,0:T(8,128)S(1)} async-done(((f32[16,32,128]{2,1,0:T(8,128)}), f32[16,32,128]{2,1,0:T(8,128)S(1)}, u32[]{:S(2)}, u32[]{:S(2)}) %all-to-all-start.3) | async-done | bytes 262176 | tf_op jit(solution)/shard_map/all_to_all | solution.py:25
  140.5 1.3 multiply_reduce_fusion
  (48 shorter events, 11.9 us)
Async XLA Ops:
  0.6 4.0 %copy-start = (bf16[1,256,2048]{2,1,0:T(8,128)(2,1)S(1)}, bf16[1,256,2048]{2,1,0:T(8,128)(2,1)}, u32[]{:S(2)}) copy-start(bf16[1,256,2048]{2,1,0:T(8,128)(2,1)} %param.7) | copy-start | bytes 3145732
  6.7 89.7 %collective-permute-start.3 = (bf16[2048,128]{1,0:T(8,128)(2,1)}, bf16[2048,128]{1,0:T(8,128)(2,1)S(1)}, u32[]{:S(2)}, u32[]{:S(2)}) collective-permute-start(bf16[2048,128]{1,0:T(8,128)(2,1)} %fusion.3), channel_id=1, source_target_pairs={{0,64},{64,0},{128,192},{192,128},{256,320},{320,256},{384,448},{4... | collective-permute-start | bytes 1572872 | tf_op jit(solution)/shard_map/ppermute | solution.py:30
  24.8 71.6 %collective-permute-start.4 = (bf16[2048,128]{1,0:T(8,128)(2,1)}, bf16[2048,128]{1,0:T(8,128)(2,1)S(1)}, u32[]{:S(2)}, u32[]{:S(2)}) collective-permute-start(bf16[2048,128]{1,0:T(8,128)(2,1)} %fusion.4), channel_id=1, source_target_pairs={{0,128},{64,192},{128,0},{192,64},{256,384},{320,448},{384,256},{4... | collective-permute-start | bytes 1572872 | tf_op jit(solution)/shard_map/ppermute | solution.py:30
  27.4 11.3 %copy-start.4 = (bf16[32]{0:T(256)(128)(2,1)S(1)}, bf16[32]{0:T(256)(128)(2,1)}, u32[]{:S(2)}) copy-start(bf16[32]{0:T(256)(128)(2,1)} %param.10) | copy-start | bytes 196
  28.9 67.6 %collective-permute-start.5 = (bf16[2048,128]{1,0:T(8,128)(2,1)}, bf16[2048,128]{1,0:T(8,128)(2,1)S(1)}, u32[]{:S(2)}, u32[]{:S(2)}) collective-permute-start(bf16[2048,128]{1,0:T(8,128)(2,1)} %fusion.5), channel_id=1, source_target_pairs={{0,192},{64,128},{128,64},{192,0},{256,448},{320,384},{384,320},{4... | collective-permute-start | bytes 1572872 | tf_op jit(solution)/shard_map/ppermute | solution.py:30
  33.7 20.5 %all-to-all-start = ((f32[16,1,128]{2,1,0:T(1,128)}), f32[16,1,128]{2,1,0:T(1,128)S(1)}, u32[]{:S(2)}, u32[]{:S(2)}) async-start(f32[16,1,128]{2,1,0:T(1,128)} %broadcast_in_dim.44), calls=%async_computation | async-start | bytes 16384 | tf_op jit(solution)/shard_map/all_to_all | solution.py:25
  55.2 31.8 %all-to-all-start.1 = ((bf16[64,35,128]{2,1,0:T(8,128)(2,1)}), bf16[64,35,128]{2,1,0:T(8,128)(2,1)S(1)}, u32[]{:S(2)}, u32[]{:S(2)}) async-start(bf16[64,35,128]{2,1,0:T(8,128)(2,1)} %broadcast_in_dim.45), calls=%async_computation.1 | async-start | bytes 1310720 | tf_op jit(solution)/shard_map/all_to_all | solution.py:25
  68.4 1.2 copy-start.1
  87.8 41.0 %collective-permute-start.2 = (bf16[2048,128]{1,0:T(8,128)(2,1)}, bf16[2048,128]{1,0:T(8,128)(2,1)}, u32[]{:S(2)}, u32[]{:S(2)}) collective-permute-start(bf16[2048,128]{1,0:T(8,128)(2,1)} %bitcast.3), channel_id=1, source_target_pairs={{0,64},{64,0},{128,192},{192,128},{256,320},{320,256},{384,448},{4... | collective-permute-start | bytes 1572872 | tf_op jit(solution)/shard_map/ppermute | solution.py:30
  93.3 16.3 %collective-permute-start = (bf16[2048,128]{1,0:T(8,128)(2,1)}, bf16[2048,128]{1,0:T(8,128)(2,1)}, u32[]{:S(2)}, u32[]{:S(2)}) collective-permute-start(bf16[2048,128]{1,0:T(8,128)(2,1)} %bitcast.3), channel_id=1, source_target_pairs={{0,128},{64,192},{128,0},{192,64},{256,384},{320,448},{384,256},{4... | collective-permute-start | bytes 1572872 | tf_op jit(solution)/shard_map/ppermute | solution.py:30
  98.3 6.3 %copy-start.2 = (bf16[1,256,2048]{2,1,0:T(8,128)(2,1)S(1)}, bf16[1,256,2048]{2,1,0:T(8,128)(2,1)}, u32[]{:S(2)}) copy-start(bf16[1,256,2048]{2,1,0:T(8,128)(2,1)} %param.7) | copy-start | bytes 3145732
  98.3 23.1 %all-to-all-start.2 = ((bf16[64,32,128]{2,1,0:T(8,128)(2,1)}), bf16[64,32,128]{2,1,0:T(8,128)(2,1)S(1)}, u32[]{:S(2)}, u32[]{:S(2)}) async-start(bf16[64,32,128]{2,1,0:T(8,128)(2,1)} %bitcast.14), calls=%async_computation.2 | async-start | bytes 1048576 | tf_op jit(solution)/shard_map/all_to_all | solution.py:126
  109.6 20.8 %collective-permute-start.1 = (bf16[2048,128]{1,0:T(8,128)(2,1)}, bf16[2048,128]{1,0:T(8,128)(2,1)S(1)}, u32[]{:S(2)}, u32[]{:S(2)}) collective-permute-start(bf16[2048,128]{1,0:T(8,128)(2,1)} %collective-permute-done), channel_id=1, source_target_pairs={{0,64},{64,0},{128,192},{192,128},{256,320},{320,256},{384,448},{4... | collective-permute-start | bytes 1572872 | tf_op jit(solution)/shard_map/ppermute | solution.py:30
  122.2 18.2 %all-to-all-start.3 = ((f32[16,32,128]{2,1,0:T(8,128)}), f32[16,32,128]{2,1,0:T(8,128)S(1)}, u32[]{:S(2)}, u32[]{:S(2)}) async-start(f32[16,32,128]{2,1,0:T(8,128)} %broadcast_in_dim.50), calls=%async_computation.3 | async-start | bytes 524288 | tf_op jit(solution)/shard_map/all_to_all | solution.py:25
  131.1 9.4 %copy-start.3 = (bf16[32,512]{1,0:T(8,128)(2,1)S(1)}, bf16[32,512]{1,0:T(8,128)(2,1)}, u32[]{:S(2)}) copy-start(bf16[32,512]{1,0:T(8,128)(2,1)} %param.9) | copy-start | bytes 98308

commit v5 on v4

--- a/solution.py
+++ b/solution.py
@@ -16,7 +16,7 @@
 GROUP = 4
 LANES = 128
 DIGIT = 64.0
-STEP = 128
+STEP = 4
 
 
 def from_all(value, axes):
@@ -25,43 +25,53 @@
     return lax.all_to_all(copies, axes, 0, 0, tiled=True)
 
 
-def to_peer(value, flip):
+def to_peer(value, flip, upward=False):
     count = lax.axis_size(REPLICA)
-    return lax.ppermute(value, REPLICA, [(i, i ^ flip) for i in range(count)])
+    return lax.ppermute(value, REPLICA, [(i, peer_of(i, flip, upward, count)) for i in range(count)])
 
 
-def combine(count, rewards_ref, filled_ref, kept_ref, *refs):
+def peer_of(member, flip, upward, count):
+    if upward and flip & 2:
+        member = (member + (2 if member & 2 else -2)) % count
+        return member ^ (flip & 1)
+    return member ^ flip
+
+
+def combine(count, rewards_ref, filled_ref, kept_ref, core_ref, *refs):
     *got_refs, out_ref = refs
-    width, _ = out_ref.shape
-    extra_rows = filled_ref.shape[1] - 3
-    digits = filled_ref[:, extra_rows:, :].astype(jnp.float32).sum(axis=0)
+    blocks, rows_own, _ = out_ref.shape
+    half = rows_own // 2
+    digits = filled_ref[:, rows_own:, :].astype(jnp.float32).sum(axis=0)
     sums = DIGIT * digits[1:2] + digits[2:3]
     average = sums[0, 0] / count
-    scales = [rewards_ref[flip] - average for flip in range(GROUP)]
+    scales = [rewards_ref[k] - average for k in range(6)]
 
     def block(step, carry):
-        rows = pl.ds(step * STEP, STEP)
-        chip = scales[0] * kept_ref[rows, :]
-        for flip in range(1, GROUP):
-            chip += scales[flip] * got_refs[flip - 1][rows, :].astype(jnp.float32)
-        out_ref[rows, :] = chip.astype(out_ref.dtype)
+        some = pl.ds(step * STEP, STEP)
+        for upward in range(2):
+            rows = pl.ds(upward * half, half)
+            chip = scales[0] * kept_ref[some, rows, :]
+            chip += scales[1] * core_ref[some, rows, :].astype(jnp.float32)
+            for k in range(2):
+                part = got_refs[2 * k + upward][some].astype(jnp.float32)
+                chip += scales[2 + 2 * k + upward] * part
+            out_ref[some, rows, :] = chip.astype(out_ref.dtype)
         return carry
 
-    lax.fori_loop(0, width // STEP, block, 0)
+    lax.fori_loop(0, blocks // STEP, block, 0)
 
 
 def combined(rewards, filled, parts, count):
-    width, quarter = parts[0].shape
+    shape = parts[0].shape
     vmem = pl.BlockSpec(memory_space=pltpu.VMEM)
+    size = shape[0] * shape[1] * shape[2]
     return pl.pallas_call(
         functools.partial(combine, count),
-        out_shape=jax.ShapeDtypeStruct((width, quarter), jnp.bfloat16),
-        in_specs=[pl.BlockSpec(memory_space=pltpu.SMEM), *([vmem] * (1 + GROUP))],
+        out_shape=jax.ShapeDtypeStruct(shape, jnp.bfloat16),
+        in_specs=[pl.BlockSpec(memory_space=pltpu.SMEM), *([vmem] * (1 + len(parts)))],
         out_specs=vmem,
         compiler_params=pltpu.CompilerParams(vmem_limit_bytes=16 * 2**20),
-        cost_estimate=pl.CostEstimate(
-            flops=8 * width * quarter, bytes_accessed=12 * width * quarter, transcendentals=0
-        ),
+        cost_estimate=pl.CostEstimate(flops=8 * size, bytes_accessed=12 * size, transcendentals=0),
         name="combine",
     )(rewards, filled, *parts)
 
@@ -81,9 +91,9 @@
     stats = jnp.concatenate([reward, reward * reward, response_len.astype(jnp.float32)])
     stats = from_all(jnp.pad(stats, (0, LANES - 3)), REPLICA)
     others = jnp.arange(replicas)
-    rewards = jnp.stack(
-        [jnp.sum(jnp.where(others == member ^ flip, stats[:, 0], 0.0)) for flip in range(GROUP)]
-    )
+    rises = jnp.where(member & 2 == 0, member - 2, member + 2) % replicas
+    peers = (member, member ^ 1, member ^ 2, rises, member ^ 3, rises ^ 1)
+    rewards = jnp.stack([jnp.sum(jnp.where(others == k, stats[:, 0], 0.0)) for k in peers])
     sums = stats.sum(axis=0)
     high = jnp.floor(sums / DIGIT)
     low = sums - DIGIT * high
@@ -116,13 +126,18 @@
 
         return with_unit(coarse) + with_unit(fine)
 
-    got = {}
-    for flip in (3, 2, 1):
-        got[flip] = to_peer(product(flip).astype(jnp.bfloat16), flip)
-    got[0] = lax.optimization_barrier(product(0))
+    got = []
+    for flip in (3, 2):
+        made = product(flip).astype(jnp.bfloat16).reshape(fsdp, 2, rows_own // 2, quarter)
+        halves = [made[:, 0], made[:, 1]]
+        swapped = [to_peer(half, flip, upward=bool(k)) for k, half in enumerate(halves)]
+        got = [*swapped, *got]
+    blocks = (fsdp, rows_own, quarter)
+    made = product(1).astype(jnp.bfloat16).reshape(blocks)
+    across = to_peer(made, 1)
+    kept = lax.optimization_barrier(product(0).reshape(blocks))
 
-    chip = combined(rewards, filled, [got[flip] for flip in range(GROUP)], count)
-    chip = chip.reshape(fsdp, rows_own, quarter)
+    chip = combined(rewards, filled, [kept, across, *got], count)
     plane = lax.all_to_all(chip, FSDP, 0, 0, tiled=True)
     plane = plane.astype(jnp.float32).sum(axis=0)
     every = from_all(plane, REPLICA)

time: 143 us -> 133 us (0.930)
  waiting for transfers between devices: 45 us -> 22.4 us
  starting transfers between devices: 62.7 us -> 72.5 us
  local copies, waits for them, and re-layouts: 6.02 us -> 11 us
  other arithmetic: 7.73 us -> 5.08 us
    all_to_all x3, waiting for transfers between devices: 37.3 us -> 15 us  [from_all(): return lax.all_to_all(copies, axes, 0, 0, tiled=True)]
    all_to_all x3, starting transfers between devices: 24.1 us -> 38.6 us  [from_all(): return lax.all_to_all(copies, axes, 0, 0, tiled=True)]
    ppermute x6 -> x8, starting transfers between devices: 32.5 us -> 27.9 us  [to_peer(): lax.ppermute(value, REPLICA, [(i, peer_of(i, flip, upward, count)) for i...]
    another operation x0 -> x1, local copies, waits for them, and re-layouts: none -> 3.89 us  [shards(): jnp.stack([jnp.sum(jnp.where(others == k, stats[:, 0], 0.0)) for k in pee...]
    another operation x1 -> x0, other arithmetic: 2.63 us -> none  [shards(): jnp.stack([jnp.sum(jnp.where(others == member ^ flip, stats[:, 0], 0.0))...]
    squeeze x0 -> x2, local copies, waits for them, and re-layouts: none -> 1.66 us  [shards(): halves = [made[:, 0], made[:, 1]]]
  transfers between devices with their start and end apart: 10 -> 12, of which waited for: 4 -> 4; matrix products, arithmetic and copies ran while one was open for 14% -> 21% of each run, Pallas kernels for 1% -> 1%
where the time goes in v5:
time: 133 us; the launch traced here: 132 us
  starting transfers between devices  72.5 us (55%)
  waiting for transfers between devices  22.4 us (17%)
  matrix products  13.5 us (10%)
  local copies, waits for them, and re-layouts  11 us (8%)
  between operations  5.74 us (4%)
  other arithmetic  5.08 us (4%)
  Pallas kernels  1.91 us (1%)
    all_to_all x3, starting transfers between devices, from_all(): return lax.all_to_all(copies, axes, 0, 0, tiled=True)  38.6 us
    ppermute x8, starting transfers between devices, to_peer(): lax.ppermute(value, REPLICA, [(i, peer_of(i, flip, upward, count)) for i...  27.9 us
    all_to_all x3, waiting for transfers between devices, from_all(): return lax.all_to_all(copies, axes, 0, 0, tiled=True)  15 us
    dot_general x8, matrix products, with_unit(): jnp.einsum('td,tk->dk', rows, part, preferred_element_type=jnp.float32)  8.03 us
    all_to_all x1, waiting for transfers between devices, shards(): plane = lax.all_to_all(chip, FSDP, 0, 0, tiled=True)  7 us
    all_to_all x1, starting transfers between devices, shards(): plane = lax.all_to_all(chip, FSDP, 0, 0, tiled=True)  6 us
    dot_general x4, matrix products, shards(): jnp.dot(normed, w, preferred_element_type=jnp.float32).astype(jnp.bfloat16)  5.44 us
    another operation x1, local copies, waits for them, and re-layouts, shards(): jnp.stack([jnp.sum(jnp.where(others == k, stats[:, 0], 0.0)) for k in pee...  3.89 us
  transfers between devices with their start and end apart: 12, of which 4 were waited for; matrix products, arithmetic and copies ran while one was open for 21% of the time, Pallas kernels for 1%

profile of v5, /device:TPU:1, one launch (start us, length us, event | category | flops | bytes accessed | tf_op | source)
XLA Modules:
  0.0 132.1 jit_solution(1883706675984846947)
XLA Ops:
  2.7 18.2 %all-to-all-start = ((f32[16,1,128]{2,1,0:T(1,128)}), f32[16,1,128]{2,1,0:T(1,128)S(1)}, u32[]{:S(2)}, u32[]{:S(2)}) async-start(f32[16,1,128]{2,1,0:T(1,128)} %broadcast_in_dim.46), calls=%async_computation | async-start | bytes 16384 | tf_op jit(solution)/shard_map/all_to_all | solution.py:25
  20.9 1.5 %fusion.7 = f32[256]{0:T(256)S(1)} fusion(bf16[1,256,2048]{2,1,0:T(8,128)(2,1)} %param.7), kind=kLoop, calls=%fused_computation.15 | loop fusion | flops 1572608 | bytes 1049600 | tf_op jit(solution)/shard_map/reduce_sum | solution.py:113
  26.3 3.2 %collective-permute-start.4 = (bf16[64,16,128]{2,1,0:T(8,128)(2,1)}, bf16[64,16,128]{2,1,0:T(8,128)(2,1)S(1)}, u32[]{:S(2)}, u32[]{:S(2)}) collective-permute-start(bf16[64,16,128]{2,1,0:T(8,128)(2,1)} %get-tuple-element.27), channel_id=1, source_target_pairs={{0,128},{64,192},{128,0},{192,64},{256,384},{320,448},{384,256},{4... | collective-permute-start | bytes 786440 | tf_op jit(solution)/shard_map/ppermute | solution.py:30
  29.5 4.3 %collective-permute-start.5 = (bf16[64,16,128]{2,1,0:T(8,128)(2,1)}, bf16[64,16,128]{2,1,0:T(8,128)(2,1)S(1)}, u32[]{:S(2)}, u32[]{:S(2)}) collective-permute-start(bf16[64,16,128]{2,1,0:T(8,128)(2,1)} %get-tuple-element.26), channel_id=1, source_target_pairs={{0,896},{64,960},{128,256},{192,320},{256,128},{320,192},{384,512}... | collective-permute-start | bytes 786440 | tf_op jit(solution)/shard_map/ppermute | solution.py:30
  36.0 2.7 %collective-permute-start.6 = (bf16[64,16,128]{2,1,0:T(8,128)(2,1)}, bf16[64,16,128]{2,1,0:T(8,128)(2,1)S(1)}, u32[]{:S(2)}, u32[]{:S(2)}) collective-permute-start(bf16[64,16,128]{2,1,0:T(8,128)(2,1)} %get-tuple-element.25), channel_id=1, source_target_pairs={{0,192},{64,128},{128,64},{192,0},{256,448},{320,384},{384,320},{4... | collective-permute-start | bytes 786440 | tf_op jit(solution)/shard_map/ppermute | solution.py:30
  38.7 3.7 %collective-permute-start.7 = (bf16[64,16,128]{2,1,0:T(8,128)(2,1)}, bf16[64,16,128]{2,1,0:T(8,128)(2,1)S(1)}, u32[]{:S(2)}, u32[]{:S(2)}) collective-permute-start(bf16[64,16,128]{2,1,0:T(8,128)(2,1)} %get-tuple-element.24), channel_id=1, source_target_pairs={{0,960},{64,896},{128,320},{192,256},{256,192},{320,128},{384,576}... | collective-permute-start | bytes 786440 | tf_op jit(solution)/shard_map/ppermute | solution.py:30
  42.4 1.6 %fusion.22 = f32[2048,128]{1,0:T(8,128)} fusion(bf16[256,512]{1,0:T(8,128)(2,1)S(1)} %bitcast_select_fusion, s32[]{:T(128)S(6)} %select_n.163, bf16[1,256,2048]{2,1,0:T(8,128)(2,1)S(1)} %copy-done, f32[256]{0:T(256)S(1)} %add_rsqrt_fusion), kind=kOutput, calls=%fused_computation.47 | convolution fusion | flops 136314880 | bytes 2163716 | tf_op jit(solution)/shard_map/td,tk->dk/dot_general | solution.py:125
  45.8 13.2 %all-to-all-start.1 = ((bf16[64,35,128]{2,1,0:T(8,128)(2,1)}), bf16[64,35,128]{2,1,0:T(8,128)(2,1)S(1)}, u32[]{:S(2)}, u32[]{:S(2)}) async-start(bf16[64,35,128]{2,1,0:T(8,128)(2,1)} %broadcast_in_dim.47), calls=%async_computation.1 | async-start | bytes 1310720 | tf_op jit(solution)/shard_map/all_to_all | solution.py:25
  59.0 2.7 %fusion.3 = bf16[2048,128]{1,0:T(8,128)(2,1)} fusion(f32[2048,128]{1,0:T(8,128)} %fusion.22, bf16[256,512]{1,0:T(8,128)(2,1)S(1)} %bitcast_select_fusion, s32[]{:T(128)S(6)} %select_n.163, bf16[1,256,2048]{2,1,0:T(8,128)(2,1)S(1)} %copy-done, f32[256]{0:T(256)S(1)} %add_rsqrt_fusion), kind=kOutput, calls=%fused_computation.11 | convolution fusion | flops 137363456 | bytes 2688004 | tf_op jit(solution)/shard_map/td,tk->dk/dot_general | solution.py:125
  61.6 3.3 %collective-permute-start.3 = (bf16[64,32,128]{2,1,0:T(8,128)(2,1)}, bf16[64,32,128]{2,1,0:T(8,128)(2,1)S(1)}, u32[]{:S(2)}, u32[]{:S(2)}) collective-permute-start(bf16[64,32,128]{2,1,0:T(8,128)(2,1)} %bitcast.17), channel_id=1, source_target_pairs={{0,64},{64,0},{128,192},{192,128},{256,320},{320,256},{384,448},{4... | collective-permute-start | bytes 1572872 | tf_op jit(solution)/shard_map/ppermute | solution.py:30
  67.0 3.9 %stack.33.rewards_ref = f32[6]{0:T(128)S(1)} concatenate(f32[1]{0:T(128)} %bitcast.7, f32[1]{0:T(128)} %bitcast.8, f32[1]{0:T(128)} %bitcast.9, f32[1]{0:T(128)} %bitcast.10, f32[1]{0:T(128)} %bitcast.11, f32[1]{0:T(128)} %bitcast.12), dimensions={0} | concatenate | bytes 48 | tf_op jit(solution)/shard_map/stack | solution.py:96
  70.9 6.5 %all-to-all-done.1.filled_ref = bf16[64,35,128]{2,1,0:T(8,128)(2,1)S(1)} async-done(((bf16[64,35,128]{2,1,0:T(8,128)(2,1)}), bf16[64,35,128]{2,1,0:T(8,128)(2,1)S(1)}, u32[]{:S(2)}, u32[]{:S(2)}) %all-to-all-start.1) | async-done | bytes 573472 | tf_op jit(solution)/shard_map/all_to_all | solution.py:25
  78.3 5.7 %collective-permute-start.2 = (bf16[2048,128]{1,0:T(8,128)(2,1)}, bf16[2048,128]{1,0:T(8,128)(2,1)}, u32[]{:S(2)}, u32[]{:S(2)}) collective-permute-start(bf16[2048,128]{1,0:T(8,128)(2,1)} %bitcast.3), channel_id=1, source_target_pairs={{0,64},{64,0},{128,192},{192,128},{256,320},{320,256},{384,448},{4... | collective-permute-start | bytes 1572872 | tf_op jit(solution)/shard_map/ppermute | solution.py:30
  84.0 2.2 %collective-permute-start = (bf16[2048,128]{1,0:T(8,128)(2,1)}, bf16[2048,128]{1,0:T(8,128)(2,1)}, u32[]{:S(2)}, u32[]{:S(2)}) collective-permute-start(bf16[2048,128]{1,0:T(8,128)(2,1)} %bitcast.3), channel_id=1, source_target_pairs={{0,128},{64,192},{128,0},{192,64},{256,384},{320,448},{384,256},{4... | collective-permute-start | bytes 1572872 | tf_op jit(solution)/shard_map/ppermute | solution.py:30
  86.3 1.9 %combine.1 = bf16[64,32,128]{2,1,0:T(8,128)(2,1)} custom-call(f32[6]{0:T(128)S(1)} %stack.33.rewards_ref, bf16[64,35,128]{2,1,0:T(8,128)(2,1)S(1)} %all-to-all-done.1.filled_ref, f32[64,32,128]{2,1,0:T(8,128)S(1)} %bitcast.98, bf16[64,32,128]{2,1,0:T(8,128)(2,1)S(1)} %collective-permute-done.3.core_ref, ...), custom_call_target="tpu_custom_call" | custom-call | flops 2097152 | bytes 3145728 | tf_op jit(solution)/shard_map/combine/pallas_call | solution.py:68
  88.2 6.0 %all-to-all-start.2 = ((bf16[64,32,128]{2,1,0:T(8,128)(2,1)}), bf16[64,32,128]{2,1,0:T(8,128)(2,1)S(1)}, u32[]{:S(2)}, u32[]{:S(2)}) async-start(bf16[64,32,128]{2,1,0:T(8,128)(2,1)} %combine.1), calls=%async_computation.2 | async-start | bytes 1048576 | tf_op jit(solution)/shard_map/all_to_all | solution.py:141
  94.4 1.6 %convolution_convert_fusion = bf16[256,128]{0,1:T(8,128)(2,1)S(1)} fusion(bf16[2048,128]{1,0:T(8,128)(2,1)} %bitcast.3, bf16[1,256,2048]{2,1,0:T(8,128)(2,1)S(1)} %copy-done.2, f32[2048]{0:T(1024)S(1)} %add.97, f32[256]{0:T(256)S(1)} %add_rsqrt_fusion), kind=kOutput, calls=%fused_computation.19 | convolution fusion | flops 136347648 | bytes 1647616 | tf_op jit(solution)/shard_map/dot_general | solution.py:155
  99.7 2.8 %collective-permute-start.1 = (bf16[2048,128]{1,0:T(8,128)(2,1)}, bf16[2048,128]{1,0:T(8,128)(2,1)S(1)}, u32[]{:S(2)}, u32[]{:S(2)}) collective-permute-start(bf16[2048,128]{1,0:T(8,128)(2,1)} %collective-permute-done), channel_id=1, source_target_pairs={{0,64},{64,0},{128,192},{192,128},{256,320},{320,256},{384,448},{4... | collective-permute-start | bytes 1572872 | tf_op jit(solution)/shard_map/ppermute | solution.py:30
  102.5 1.6 %convolution_convert_fusion.2 = bf16[256,128]{0,1:T(8,128)(2,1)S(1)} fusion(bf16[2048,128]{1,0:T(8,128)(2,1)} %collective-permute-done, bf16[1,256,2048]{2,1,0:T(8,128)(2,1)S(1)} %copy-done.2, f32[2048]{0:T(1024)S(1)} %add.97, f32[256]{0:T(256)S(1)} %add_rsqrt_fusion), kind=kOutput, calls=%fused_computation.21 | convolution fusion | flops 136347648 | bytes 1647616 | tf_op jit(solution)/shard_map/dot_general | solution.py:155
  104.1 7.0 %all-to-all-done.2 = bf16[64,32,128]{2,1,0:T(8,128)(2,1)S(1)} async-done(((bf16[64,32,128]{2,1,0:T(8,128)(2,1)}), bf16[64,32,128]{2,1,0:T(8,128)(2,1)S(1)}, u32[]{:S(2)}, u32[]{:S(2)}) %all-to-all-start.2) | async-done | bytes 524320 | tf_op jit(solution)/shard_map/all_to_all | solution.py:141
  112.0 7.2 %all-to-all-start.3 = ((f32[16,32,128]{2,1,0:T(8,128)}), f32[16,32,128]{2,1,0:T(8,128)S(1)}, u32[]{:S(2)}, u32[]{:S(2)}) async-start(f32[16,32,128]{2,1,0:T(8,128)} %broadcast_in_dim.52), calls=%async_computation.3 | async-start | bytes 524288 | tf_op jit(solution)/shard_map/all_to_all | solution.py:25
  119.1 1.6 %convolution_convert_fusion.1 = bf16[256,128]{0,1:T(8,128)(2,1)S(1)} fusion(bf16[2048,128]{1,0:T(8,128)(2,1)} %collective-permute-done.2, bf16[1,256,2048]{2,1,0:T(8,128)(2,1)S(1)} %copy-done.2, f32[2048]{0:T(1024)S(1)} %add.97, f32[256]{0:T(256)S(1)} %add_rsqrt_fusion), kind=kOutput, calls=%fused_computation.20 | convolution fusion | flops 136347648 | bytes 1647616 | tf_op jit(solution)/shard_map/dot_general | solution.py:155
  122.3 8.5 %all-to-all-done.3 = f32[16,32,128]{2,1,0:T(8,128)S(1)} async-done(((f32[16,32,128]{2,1,0:T(8,128)}), f32[16,32,128]{2,1,0:T(8,128)S(1)}, u32[]{:S(2)}, u32[]{:S(2)}) %all-to-all-start.3) | async-done | bytes 262176 | tf_op jit(solution)/shard_map/all_to_all | solution.py:25
  130.8 1.3 %multiply_reduce_fusion = (f32[32]{0:T(128)}, f32[32,512]{1,0:T(8,128)}) fusion(bf16[32,512]{1,0:T(8,128)(2,1)S(1)} %copy-done.3, f32[32,128]{1,0:T(8,128)S(1)} %get-tuple-element.35, f32[32,128]{1,0:T(8,128)S(1)} %get-tuple-element.36, f32[32,128]{1,0:T(8,128)S(1)} %get-tuple-element.37, f32[32,128]{1,0:T(8,128)S(1)} %get-tuple-element.34, f32[]{:T(128)} %bitcast.29, ...), kind=kLoop, calls=%fused_computation.35 | loop fusion | flops 131040 | bytes 164100 | tf_op jit(solution)/shard_map/reduce_sum | solution.py:148
  (54 shorter events, 14.1 us)
Async XLA Ops:
  0.6 23.5 %copy-start = (bf16[1,256,2048]{2,1,0:T(8,128)(2,1)S(1)}, bf16[1,256,2048]{2,1,0:T(8,128)(2,1)}, u32[]{:S(2)}) copy-start(bf16[1,256,2048]{2,1,0:T(8,128)(2,1)} %param.7) | copy-start | bytes 3145732
  2.7 42.1 %all-to-all-start = ((f32[16,1,128]{2,1,0:T(1,128)}), f32[16,1,128]{2,1,0:T(1,128)S(1)}, u32[]{:S(2)}, u32[]{:S(2)}) async-start(f32[16,1,128]{2,1,0:T(1,128)} %broadcast_in_dim.46), calls=%async_computation | async-start | bytes 16384 | tf_op jit(solution)/shard_map/all_to_all | solution.py:25
  26.3 52.0 %collective-permute-start.4 = (bf16[64,16,128]{2,1,0:T(8,128)(2,1)}, bf16[64,16,128]{2,1,0:T(8,128)(2,1)S(1)}, u32[]{:S(2)}, u32[]{:S(2)}) collective-permute-start(bf16[64,16,128]{2,1,0:T(8,128)(2,1)} %get-tuple-element.27), channel_id=1, source_target_pairs={{0,128},{64,192},{128,0},{192,64},{256,384},{320,448},{384,256},{4... | collective-permute-start | bytes 786440 | tf_op jit(solution)/shard_map/ppermute | solution.py:30
  29.5 54.5 %collective-permute-start.5 = (bf16[64,16,128]{2,1,0:T(8,128)(2,1)}, bf16[64,16,128]{2,1,0:T(8,128)(2,1)S(1)}, u32[]{:S(2)}, u32[]{:S(2)}) collective-permute-start(bf16[64,16,128]{2,1,0:T(8,128)(2,1)} %get-tuple-element.26), channel_id=1, source_target_pairs={{0,896},{64,960},{128,256},{192,320},{256,128},{320,192},{384,512}... | collective-permute-start | bytes 786440 | tf_op jit(solution)/shard_map/ppermute | solution.py:30
  36.0 50.3 %collective-permute-start.6 = (bf16[64,16,128]{2,1,0:T(8,128)(2,1)}, bf16[64,16,128]{2,1,0:T(8,128)(2,1)S(1)}, u32[]{:S(2)}, u32[]{:S(2)}) collective-permute-start(bf16[64,16,128]{2,1,0:T(8,128)(2,1)} %get-tuple-element.25), channel_id=1, source_target_pairs={{0,192},{64,128},{128,64},{192,0},{256,448},{320,384},{384,320},{4... | collective-permute-start | bytes 786440 | tf_op jit(solution)/shard_map/ppermute | solution.py:30
  38.7 47.6 %collective-permute-start.7 = (bf16[64,16,128]{2,1,0:T(8,128)(2,1)}, bf16[64,16,128]{2,1,0:T(8,128)(2,1)S(1)}, u32[]{:S(2)}, u32[]{:S(2)}) collective-permute-start(bf16[64,16,128]{2,1,0:T(8,128)(2,1)} %get-tuple-element.24), channel_id=1, source_target_pairs={{0,960},{64,896},{128,320},{192,256},{256,192},{320,128},{384,576}... | collective-permute-start | bytes 786440 | tf_op jit(solution)/shard_map/ppermute | solution.py:30
  42.4 2.3 %copy-start.4 = (bf16[32]{0:T(256)(128)(2,1)S(1)}, bf16[32]{0:T(256)(128)(2,1)}, u32[]{:S(2)}) copy-start(bf16[32]{0:T(256)(128)(2,1)} %param.10) | copy-start | bytes 196
  45.8 31.7 %all-to-all-start.1 = ((bf16[64,35,128]{2,1,0:T(8,128)(2,1)}), bf16[64,35,128]{2,1,0:T(8,128)(2,1)S(1)}, u32[]{:S(2)}, u32[]{:S(2)}) async-start(bf16[64,35,128]{2,1,0:T(8,128)(2,1)} %broadcast_in_dim.47), calls=%async_computation.1 | async-start | bytes 1310720 | tf_op jit(solution)/shard_map/all_to_all | solution.py:25
  61.6 3.9 %copy-start.1 = (bf16[1,256,2048]{2,1,0:T(8,128)(2,1)S(1)}, bf16[1,256,2048]{2,1,0:T(8,128)(2,1)}, u32[]{:S(2)}) copy-start(bf16[1,256,2048]{2,1,0:T(8,128)(2,1)} %param.7) | copy-start | bytes 3145732
  61.6 24.6 %collective-permute-start.3 = (bf16[64,32,128]{2,1,0:T(8,128)(2,1)}, bf16[64,32,128]{2,1,0:T(8,128)(2,1)S(1)}, u32[]{:S(2)}, u32[]{:S(2)}) collective-permute-start(bf16[64,32,128]{2,1,0:T(8,128)(2,1)} %bitcast.17), channel_id=1, source_target_pairs={{0,64},{64,0},{128,192},{192,128},{256,320},{320,256},{384,448},{4... | collective-permute-start | bytes 1572872 | tf_op jit(solution)/shard_map/ppermute | solution.py:30
  78.3 40.8 %collective-permute-start.2 = (bf16[2048,128]{1,0:T(8,128)(2,1)}, bf16[2048,128]{1,0:T(8,128)(2,1)}, u32[]{:S(2)}, u32[]{:S(2)}) collective-permute-start(bf16[2048,128]{1,0:T(8,128)(2,1)} %bitcast.3), channel_id=1, source_target_pairs={{0,64},{64,0},{128,192},{192,128},{256,320},{320,256},{384,448},{4... | collective-permute-start | bytes 1572872 | tf_op jit(solution)/shard_map/ppermute | solution.py:30
  84.0 15.7 %collective-permute-start = (bf16[2048,128]{1,0:T(8,128)(2,1)}, bf16[2048,128]{1,0:T(8,128)(2,1)}, u32[]{:S(2)}, u32[]{:S(2)}) collective-permute-start(bf16[2048,128]{1,0:T(8,128)(2,1)} %bitcast.3), channel_id=1, source_target_pairs={{0,128},{64,192},{128,0},{192,64},{256,384},{320,448},{384,256},{4... | collective-permute-start | bytes 1572872 | tf_op jit(solution)/shard_map/ppermute | solution.py:30
  88.2 6.2 %copy-start.2 = (bf16[1,256,2048]{2,1,0:T(8,128)(2,1)S(1)}, bf16[1,256,2048]{2,1,0:T(8,128)(2,1)}, u32[]{:S(2)}) copy-start(bf16[1,256,2048]{2,1,0:T(8,128)(2,1)} %param.7) | copy-start | bytes 3145732
  88.2 22.9 %all-to-all-start.2 = ((bf16[64,32,128]{2,1,0:T(8,128)(2,1)}), bf16[64,32,128]{2,1,0:T(8,128)(2,1)S(1)}, u32[]{:S(2)}, u32[]{:S(2)}) async-start(bf16[64,32,128]{2,1,0:T(8,128)(2,1)} %combine.1), calls=%async_computation.2 | async-start | bytes 1048576 | tf_op jit(solution)/shard_map/all_to_all | solution.py:141
  99.7 21.0 %collective-permute-start.1 = (bf16[2048,128]{1,0:T(8,128)(2,1)}, bf16[2048,128]{1,0:T(8,128)(2,1)S(1)}, u32[]{:S(2)}, u32[]{:S(2)}) collective-permute-start(bf16[2048,128]{1,0:T(8,128)(2,1)} %collective-permute-done), channel_id=1, source_target_pairs={{0,64},{64,0},{128,192},{192,128},{256,320},{320,256},{384,448},{4... | collective-permute-start | bytes 1572872 | tf_op jit(solution)/shard_map/ppermute | solution.py:30
  112.0 18.8 %all-to-all-start.3 = ((f32[16,32,128]{2,1,0:T(8,128)}), f32[16,32,128]{2,1,0:T(8,128)S(1)}, u32[]{:S(2)}, u32[]{:S(2)}) async-start(f32[16,32,128]{2,1,0:T(8,128)} %broadcast_in_dim.52), calls=%async_computation.3 | async-start | bytes 524288 | tf_op jit(solution)/shard_map/all_to_all | solution.py:25
  121.4 9.4 %copy-start.3 = (bf16[32,512]{1,0:T(8,128)(2,1)S(1)}, bf16[32,512]{1,0:T(8,128)(2,1)}, u32[]{:S(2)}) copy-start(bf16[32,512]{1,0:T(8,128)(2,1)} %param.9) | copy-start | bytes 98308

commit v6 on v4

--- a/solution.py
+++ b/solution.py
@@ -25,25 +25,31 @@
     return lax.all_to_all(copies, axes, 0, 0, tiled=True)
 
 
-def to_peer(value, flip):
-    count = lax.axis_size(REPLICA)
-    return lax.ppermute(value, REPLICA, [(i, i ^ flip) for i in range(count)])
+def peer_of(member, peer, count):
+    if peer == 3:
+        return (member + (2 if member & 2 else -2)) % count ^ 1
+    return member ^ peer
 
 
-def combine(count, rewards_ref, filled_ref, kept_ref, *refs):
-    *got_refs, out_ref = refs
-    width, _ = out_ref.shape
+def to_peer(value, peer):
+    count = lax.axis_size(REPLICA)
+    return lax.ppermute(value, REPLICA, [(i, peer_of(i, peer, count)) for i in range(count)])
+
+
+def combine(count, rewards_ref, filled_ref, *refs):
+    *parts_refs, out_ref = refs
+    width = out_ref.shape[0]
     extra_rows = filled_ref.shape[1] - 3
     digits = filled_ref[:, extra_rows:, :].astype(jnp.float32).sum(axis=0)
     sums = DIGIT * digits[1:2] + digits[2:3]
     average = sums[0, 0] / count
-    scales = [rewards_ref[flip] - average for flip in range(GROUP)]
+    scales = [rewards_ref[k] - average for k in range(GROUP)]
 
     def block(step, carry):
         rows = pl.ds(step * STEP, STEP)
-        chip = scales[0] * kept_ref[rows, :]
-        for flip in range(1, GROUP):
-            chip += scales[flip] * got_refs[flip - 1][rows, :].astype(jnp.float32)
+        chip = scales[0] * parts_refs[0][rows, :]
+        for peer in range(1, GROUP):
+            chip += scales[peer] * parts_refs[peer][rows, :].astype(jnp.float32)
         out_ref[rows, :] = chip.astype(out_ref.dtype)
         return carry
 
@@ -80,10 +86,11 @@
     reward = reward_bucket.astype(jnp.float32)
     stats = jnp.concatenate([reward, reward * reward, response_len.astype(jnp.float32)])
     stats = from_all(jnp.pad(stats, (0, LANES - 3)), REPLICA)
-    others = jnp.arange(replicas)
-    rewards = jnp.stack(
-        [jnp.sum(jnp.where(others == member ^ flip, stats[:, 0], 0.0)) for flip in range(GROUP)]
-    )
+    above = jnp.where(member & 2 == 0, member - 2, member + 2) % replicas ^ 1
+    which = jnp.arange(GROUP)
+    peers = jnp.where(which == 3, above, member ^ which)
+    chosen = peers[:, None] == jnp.arange(replicas)[None, :]
+    rewards = jnp.sum(jnp.where(chosen, stats[:, 0][None, :], 0.0), axis=1)
     sums = stats.sum(axis=0)
     high = jnp.floor(sums / DIGIT)
     low = sums - DIGIT * high
@@ -116,12 +123,13 @@
 
         return with_unit(coarse) + with_unit(fine)
 
-    got = {}
-    for flip in (3, 2, 1):
-        got[flip] = to_peer(product(flip).astype(jnp.bfloat16), flip)
-    got[0] = lax.optimization_barrier(product(0))
+    parts = {}
+    for peer in (3, 2, 1):
+        made = product(peer).astype(jnp.bfloat16)
+        parts[peer] = to_peer(made, peer)
+    parts[0] = lax.optimization_barrier(product(0))
 
-    chip = combined(rewards, filled, [got[flip] for flip in range(GROUP)], count)
+    chip = combined(rewards, filled, [parts[peer] for peer in range(GROUP)], count)
     chip = chip.reshape(fsdp, rows_own, quarter)
     plane = lax.all_to_all(chip, FSDP, 0, 0, tiled=True)
     plane = plane.astype(jnp.float32).sum(axis=0)

time: 143 us -> 137 us (0.958)
  waiting for transfers between devices: 45 us -> 41.4 us
  other arithmetic: 7.73 us -> 4.65 us
    all_to_all x3, waiting for transfers between devices: 37.3 us -> 33.6 us  [from_all(): return lax.all_to_all(copies, axes, 0, 0, tiled=True)]
    another operation x1 -> x0, other arithmetic: 2.63 us -> none  [shards(): jnp.stack([jnp.sum(jnp.where(others == member ^ flip, stats[:, 0], 0.0))...]
  transfers between devices with their start and end apart: 10 -> 10, of which waited for: 4 -> 5; matrix products, arithmetic and copies ran while one was open for 14% -> 12% of each run, Pallas kernels for 1% -> 1%
where the time goes in v6:
time: 137 us; the launch traced here: 136 us
  starting transfers between devices  63.2 us (46%)
  waiting for transfers between devices  41.4 us (30%)
  matrix products  12.9 us (9%)
  local copies, waits for them, and re-layouts  6.02 us (4%)
  between operations  5.59 us (4%)
  other arithmetic  4.65 us (3%)
  Pallas kernels  1.9 us (1%)
    all_to_all x3, waiting for transfers between devices, from_all(): return lax.all_to_all(copies, axes, 0, 0, tiled=True)  33.6 us
    ppermute x6, starting transfers between devices, to_peer(): lax.ppermute(value, REPLICA, [(i, peer_of(i, peer, count)) for i in range...  32.4 us
    all_to_all x3, starting transfers between devices, from_all(): return lax.all_to_all(copies, axes, 0, 0, tiled=True)  24.8 us
    dot_general x8, matrix products, with_unit(): jnp.einsum('td,tk->dk', rows, part, preferred_element_type=jnp.float32)  7.47 us
    all_to_all x1, waiting for transfers between devices, shards(): plane = lax.all_to_all(chip, FSDP, 0, 0, tiled=True)  7.22 us
    all_to_all x1, starting transfers between devices, shards(): plane = lax.all_to_all(chip, FSDP, 0, 0, tiled=True)  6.12 us
    dot_general x4, matrix products, shards(): jnp.dot(normed, w, preferred_element_type=jnp.float32).astype(jnp.bfloat16)  5.44 us
  transfers between devices with their start and end apart: 10, of which 5 were waited for; matrix products, arithmetic and copies ran while one was open for 12% of the time, Pallas kernels for 1%

profile of v6, /device:TPU:1, one launch (start us, length us, event | category | flops | bytes accessed | tf_op | source)
XLA Modules:
  0.0 135.7 jit_solution(1479523487620064564)
XLA Ops:
  0.7 1.6 %fusion.7 = f32[256]{0:T(256)S(1)} fusion(bf16[1,256,2048]{2,1,0:T(8,128)(2,1)} %param.7), kind=kLoop, calls=%fused_computation.15 | loop fusion | flops 1572608 | bytes 1049600 | tf_op jit(solution)/shard_map/reduce_sum | solution.py:110
  3.6 1.1 bitcast_select_fusion
  5.3 1.4 %fusion.3 = bf16[2048,128]{1,0:T(8,128)(2,1)} fusion(f32[2048,128]{1,0:T(8,128)S(1)} %fusion.22, bf16[256,512]{1,0:T(8,128)(2,1)S(1)} %bitcast_select_fusion, s32[]{:T(128)S(6)} %select_n.152, bf16[1,256,2048]{2,1,0:T(8,128)(2,1)S(1)} %copy-done, f32[256]{0:T(256)S(1)} %add_rsqrt_fusion), kind=kOutput, calls=%fused_computation.11 | convolution fusion | flops 137363456 | bytes 2688004 | tf_op jit(solution)/shard_map/td,tk->dk/dot_general | solution.py:122
  6.7 16.0 %collective-permute-start.3 = (bf16[2048,128]{1,0:T(8,128)(2,1)}, bf16[2048,128]{1,0:T(8,128)(2,1)S(1)}, u32[]{:S(2)}, u32[]{:S(2)}) collective-permute-start(bf16[2048,128]{1,0:T(8,128)(2,1)} %fusion.3), channel_id=1, source_target_pairs={{0,64},{64,0},{128,192},{192,128},{256,320},{320,256},{384,448},{4... | collective-permute-start | bytes 1572872 | tf_op jit(solution)/shard_map/ppermute | solution.py:36
  23.4 1.4 %fusion.4 = bf16[2048,128]{1,0:T(8,128)(2,1)} fusion(f32[2048,128]{1,0:T(8,128)S(1)} %fusion.19, bf16[256,512]{1,0:T(8,128)(2,1)S(1)} %bitcast_select_fusion, s32[]{:T(128)S(6)} %select_n.153, bf16[1,256,2048]{2,1,0:T(8,128)(2,1)S(1)} %copy-done, f32[256]{0:T(256)S(1)} %add_rsqrt_fusion), kind=kOutput, calls=%fused_computation.12 | convolution fusion | flops 137363456 | bytes 2688004 | tf_op jit(solution)/shard_map/td,tk->dk/dot_general | solution.py:122
  24.8 1.9 %collective-permute-start.4 = (bf16[2048,128]{1,0:T(8,128)(2,1)}, bf16[2048,128]{1,0:T(8,128)(2,1)S(1)}, u32[]{:S(2)}, u32[]{:S(2)}) collective-permute-start(bf16[2048,128]{1,0:T(8,128)(2,1)} %fusion.4), channel_id=1, source_target_pairs={{0,128},{64,192},{128,0},{192,64},{256,384},{320,448},{384,256},{4... | collective-permute-start | bytes 1572872 | tf_op jit(solution)/shard_map/ppermute | solution.py:36
  27.4 1.4 %fusion.5 = bf16[2048,128]{1,0:T(8,128)(2,1)} fusion(f32[2048,128]{1,0:T(8,128)S(1)} %fusion.16, bf16[256,512]{1,0:T(8,128)(2,1)S(1)} %bitcast_select_fusion, s32[]{:T(128)S(6)} %select_n.154, bf16[1,256,2048]{2,1,0:T(8,128)(2,1)S(1)} %copy-done, f32[256]{0:T(256)S(1)} %add_rsqrt_fusion), kind=kOutput, calls=%fused_computation.13 | convolution fusion | flops 137363456 | bytes 2688004 | tf_op jit(solution)/shard_map/td,tk->dk/dot_general | solution.py:122
  28.9 4.3 %collective-permute-start.5 = (bf16[2048,128]{1,0:T(8,128)(2,1)}, bf16[2048,128]{1,0:T(8,128)(2,1)S(1)}, u32[]{:S(2)}, u32[]{:S(2)}) collective-permute-start(bf16[2048,128]{1,0:T(8,128)(2,1)} %fusion.5), channel_id=1, source_target_pairs={{0,960},{64,896},{128,320},{192,256},{256,192},{320,128},{384,576}... | collective-permute-start | bytes 1572872 | tf_op jit(solution)/shard_map/ppermute | solution.py:36
  34.5 4.4 %all-to-all-start = ((f32[16,1,128]{2,1,0:T(1,128)}), f32[16,1,128]{2,1,0:T(1,128)S(1)}, u32[]{:S(2)}, u32[]{:S(2)}) async-start(f32[16,1,128]{2,1,0:T(1,128)} %broadcast_in_dim.57), calls=%async_computation | async-start | bytes 16384 | tf_op jit(solution)/shard_map/all_to_all | solution.py:25
  39.6 8.7 %all-to-all-done = f32[16,1,128]{2,1,0:T(1,128)S(1)} async-done(((f32[16,1,128]{2,1,0:T(1,128)}), f32[16,1,128]{2,1,0:T(1,128)S(1)}, u32[]{:S(2)}, u32[]{:S(2)}) %all-to-all-start) | async-done | bytes 8224 | tf_op jit(solution)/shard_map/all_to_all | solution.py:25
  49.3 13.2 %all-to-all-start.1 = ((bf16[64,35,128]{2,1,0:T(8,128)(2,1)}), bf16[64,35,128]{2,1,0:T(8,128)(2,1)S(1)}, u32[]{:S(2)}, u32[]{:S(2)}) async-start(bf16[64,35,128]{2,1,0:T(8,128)(2,1)} %broadcast_in_dim.58), calls=%async_computation.1 | async-start | bytes 1310720 | tf_op jit(solution)/shard_map/all_to_all | solution.py:25
  64.7 16.4 %all-to-all-done.1.filled_ref = bf16[64,35,128]{2,1,0:T(8,128)(2,1)S(1)} async-done(((bf16[64,35,128]{2,1,0:T(8,128)(2,1)}), bf16[64,35,128]{2,1,0:T(8,128)(2,1)S(1)}, u32[]{:S(2)}, u32[]{:S(2)}) %all-to-all-start.1) | async-done | bytes 573472 | tf_op jit(solution)/shard_map/all_to_all | solution.py:25
  82.0 5.5 %collective-permute-start.2 = (bf16[2048,128]{1,0:T(8,128)(2,1)}, bf16[2048,128]{1,0:T(8,128)(2,1)}, u32[]{:S(2)}, u32[]{:S(2)}) collective-permute-start(bf16[2048,128]{1,0:T(8,128)(2,1)} %bitcast.3), channel_id=1, source_target_pairs={{0,64},{64,0},{128,192},{192,128},{256,320},{320,256},{384,448},{4... | collective-permute-start | bytes 1572872 | tf_op jit(solution)/shard_map/ppermute | solution.py:36
  87.4 1.9 %collective-permute-start = (bf16[2048,128]{1,0:T(8,128)(2,1)}, bf16[2048,128]{1,0:T(8,128)(2,1)}, u32[]{:S(2)}, u32[]{:S(2)}) collective-permute-start(bf16[2048,128]{1,0:T(8,128)(2,1)} %bitcast.3), channel_id=1, source_target_pairs={{0,128},{64,192},{128,0},{192,64},{256,384},{320,448},{384,256},{4... | collective-permute-start | bytes 1572872 | tf_op jit(solution)/shard_map/ppermute | solution.py:36
  89.4 1.9 %combine.1 = bf16[2048,128]{1,0:T(8,128)(2,1)} custom-call(f32[4]{0:T(128)S(1)} %select_reduce_fusion.rewards_ref, bf16[64,35,128]{2,1,0:T(8,128)(2,1)S(1)} %all-to-all-done.1.filled_ref, f32[2048,128]{1,0:T(8,128)S(1)} %convolution_add_fusion.3.refs_0_, bf16[2048,128]{1,0:T(8,128)(2,1)S(1)} %collective-permute-done.3.refs_1_, ...), custom_call_target="tpu_custom_call" | custom-call | flops 2097152 | bytes 3145728 | tf_op jit(solution)/shard_map/combine/pallas_call | solution.py:62
  91.3 6.1 %all-to-all-start.2 = ((bf16[64,32,128]{2,1,0:T(8,128)(2,1)}), bf16[64,32,128]{2,1,0:T(8,128)(2,1)S(1)}, u32[]{:S(2)}, u32[]{:S(2)}) async-start(bf16[64,32,128]{2,1,0:T(8,128)(2,1)} %bitcast.10), calls=%async_computation.2 | async-start | bytes 1048576 | tf_op jit(solution)/shard_map/all_to_all | solution.py:134
  97.6 1.6 %convolution_convert_fusion = bf16[256,128]{0,1:T(8,128)(2,1)S(1)} fusion(bf16[2048,128]{1,0:T(8,128)(2,1)} %bitcast.3, bf16[1,256,2048]{2,1,0:T(8,128)(2,1)S(1)} %copy-done.2, f32[2048]{0:T(1024)S(1)} %add.97, f32[256]{0:T(256)S(1)} %add_rsqrt_fusion), kind=kOutput, calls=%fused_computation.19 | convolution fusion | flops 136347648 | bytes 1647616 | tf_op jit(solution)/shard_map/dot_general | solution.py:148
  103.1 2.8 %collective-permute-start.1 = (bf16[2048,128]{1,0:T(8,128)(2,1)}, bf16[2048,128]{1,0:T(8,128)(2,1)S(1)}, u32[]{:S(2)}, u32[]{:S(2)}) collective-permute-start(bf16[2048,128]{1,0:T(8,128)(2,1)} %collective-permute-done), channel_id=1, source_target_pairs={{0,64},{64,0},{128,192},{192,128},{256,320},{320,256},{384,448},{4... | collective-permute-start | bytes 1572872 | tf_op jit(solution)/shard_map/ppermute | solution.py:36
  105.9 1.6 %convolution_convert_fusion.2 = bf16[256,128]{0,1:T(8,128)(2,1)S(1)} fusion(bf16[2048,128]{1,0:T(8,128)(2,1)} %collective-permute-done, bf16[1,256,2048]{2,1,0:T(8,128)(2,1)S(1)} %copy-done.2, f32[2048]{0:T(1024)S(1)} %add.97, f32[256]{0:T(256)S(1)} %add_rsqrt_fusion), kind=kOutput, calls=%fused_computation.21 | convolution fusion | flops 136347648 | bytes 1647616 | tf_op jit(solution)/shard_map/dot_general | solution.py:148
  107.5 7.2 %all-to-all-done.2 = bf16[64,32,128]{2,1,0:T(8,128)(2,1)S(1)} async-done(((bf16[64,32,128]{2,1,0:T(8,128)(2,1)}), bf16[64,32,128]{2,1,0:T(8,128)(2,1)S(1)}, u32[]{:S(2)}, u32[]{:S(2)}) %all-to-all-start.2) | async-done | bytes 524320 | tf_op jit(solution)/shard_map/all_to_all | solution.py:134
  115.6 7.1 %all-to-all-start.3 = ((f32[16,32,128]{2,1,0:T(8,128)}), f32[16,32,128]{2,1,0:T(8,128)S(1)}, u32[]{:S(2)}, u32[]{:S(2)}) async-start(f32[16,32,128]{2,1,0:T(8,128)} %broadcast_in_dim.66), calls=%async_computation.3 | async-start | bytes 524288 | tf_op jit(solution)/shard_map/all_to_all | solution.py:25
  122.7 1.6 %convolution_convert_fusion.1 = bf16[256,128]{0,1:T(8,128)(2,1)S(1)} fusion(bf16[2048,128]{1,0:T(8,128)(2,1)} %collective-permute-done.2, bf16[1,256,2048]{2,1,0:T(8,128)(2,1)S(1)} %copy-done.2, f32[2048]{0:T(1024)S(1)} %add.97, f32[256]{0:T(256)S(1)} %add_rsqrt_fusion), kind=kOutput, calls=%fused_computation.20 | convolution fusion | flops 136347648 | bytes 1647616 | tf_op jit(solution)/shard_map/dot_general | solution.py:148
  125.8 8.5 %all-to-all-done.3 = f32[16,32,128]{2,1,0:T(8,128)S(1)} async-done(((f32[16,32,128]{2,1,0:T(8,128)}), f32[16,32,128]{2,1,0:T(8,128)S(1)}, u32[]{:S(2)}, u32[]{:S(2)}) %all-to-all-start.3) | async-done | bytes 262176 | tf_op jit(solution)/shard_map/all_to_all | solution.py:25
  134.3 1.3 multiply_reduce_fusion
  (48 shorter events, 11.0 us)
Async XLA Ops:
  0.6 4.0 %copy-start = (bf16[1,256,2048]{2,1,0:T(8,128)(2,1)S(1)}, bf16[1,256,2048]{2,1,0:T(8,128)(2,1)}, u32[]{:S(2)}) copy-start(bf16[1,256,2048]{2,1,0:T(8,128)(2,1)} %param.7) | copy-start | bytes 3145732
  6.7 82.6 %collective-permute-start.3 = (bf16[2048,128]{1,0:T(8,128)(2,1)}, bf16[2048,128]{1,0:T(8,128)(2,1)S(1)}, u32[]{:S(2)}, u32[]{:S(2)}) collective-permute-start(bf16[2048,128]{1,0:T(8,128)(2,1)} %fusion.3), channel_id=1, source_target_pairs={{0,64},{64,0},{128,192},{192,128},{256,320},{320,256},{384,448},{4... | collective-permute-start | bytes 1572872 | tf_op jit(solution)/shard_map/ppermute | solution.py:36
  24.8 64.5 %collective-permute-start.4 = (bf16[2048,128]{1,0:T(8,128)(2,1)}, bf16[2048,128]{1,0:T(8,128)(2,1)S(1)}, u32[]{:S(2)}, u32[]{:S(2)}) collective-permute-start(bf16[2048,128]{1,0:T(8,128)(2,1)} %fusion.4), channel_id=1, source_target_pairs={{0,128},{64,192},{128,0},{192,64},{256,384},{320,448},{384,256},{4... | collective-permute-start | bytes 1572872 | tf_op jit(solution)/shard_map/ppermute | solution.py:36
  27.4 12.2 %copy-start.4 = (bf16[32]{0:T(256)(128)(2,1)S(1)}, bf16[32]{0:T(256)(128)(2,1)}, u32[]{:S(2)}) copy-start(bf16[32]{0:T(256)(128)(2,1)} %param.10) | copy-start | bytes 196
  28.9 60.5 %collective-permute-start.5 = (bf16[2048,128]{1,0:T(8,128)(2,1)}, bf16[2048,128]{1,0:T(8,128)(2,1)S(1)}, u32[]{:S(2)}, u32[]{:S(2)}) collective-permute-start(bf16[2048,128]{1,0:T(8,128)(2,1)} %fusion.5), channel_id=1, source_target_pairs={{0,960},{64,896},{128,320},{192,256},{256,192},{320,128},{384,576}... | collective-permute-start | bytes 1572872 | tf_op jit(solution)/shard_map/ppermute | solution.py:36
  34.5 13.8 %all-to-all-start = ((f32[16,1,128]{2,1,0:T(1,128)}), f32[16,1,128]{2,1,0:T(1,128)S(1)}, u32[]{:S(2)}, u32[]{:S(2)}) async-start(f32[16,1,128]{2,1,0:T(1,128)} %broadcast_in_dim.57), calls=%async_computation | async-start | bytes 16384 | tf_op jit(solution)/shard_map/all_to_all | solution.py:25
  49.3 31.8 %all-to-all-start.1 = ((bf16[64,35,128]{2,1,0:T(8,128)(2,1)}), bf16[64,35,128]{2,1,0:T(8,128)(2,1)S(1)}, u32[]{:S(2)}, u32[]{:S(2)}) async-start(bf16[64,35,128]{2,1,0:T(8,128)(2,1)} %broadcast_in_dim.58), calls=%async_computation.1 | async-start | bytes 1310720 | tf_op jit(solution)/shard_map/all_to_all | solution.py:25
  62.5 1.2 copy-start.1
  82.0 40.7 %collective-permute-start.2 = (bf16[2048,128]{1,0:T(8,128)(2,1)}, bf16[2048,128]{1,0:T(8,128)(2,1)}, u32[]{:S(2)}, u32[]{:S(2)}) collective-permute-start(bf16[2048,128]{1,0:T(8,128)(2,1)} %bitcast.3), channel_id=1, source_target_pairs={{0,64},{64,0},{128,192},{192,128},{256,320},{320,256},{384,448},{4... | collective-permute-start | bytes 1572872 | tf_op jit(solution)/shard_map/ppermute | solution.py:36
  87.4 15.7 %collective-permute-start = (bf16[2048,128]{1,0:T(8,128)(2,1)}, bf16[2048,128]{1,0:T(8,128)(2,1)}, u32[]{:S(2)}, u32[]{:S(2)}) collective-permute-start(bf16[2048,128]{1,0:T(8,128)(2,1)} %bitcast.3), channel_id=1, source_target_pairs={{0,128},{64,192},{128,0},{192,64},{256,384},{320,448},{384,256},{4... | collective-permute-start | bytes 1572872 | tf_op jit(solution)/shard_map/ppermute | solution.py:36
  91.3 6.3 %copy-start.2 = (bf16[1,256,2048]{2,1,0:T(8,128)(2,1)S(1)}, bf16[1,256,2048]{2,1,0:T(8,128)(2,1)}, u32[]{:S(2)}) copy-start(bf16[1,256,2048]{2,1,0:T(8,128)(2,1)} %param.7) | copy-start | bytes 3145732
  91.3 23.4 %all-to-all-start.2 = ((bf16[64,32,128]{2,1,0:T(8,128)(2,1)}), bf16[64,32,128]{2,1,0:T(8,128)(2,1)S(1)}, u32[]{:S(2)}, u32[]{:S(2)}) async-start(bf16[64,32,128]{2,1,0:T(8,128)(2,1)} %bitcast.10), calls=%async_computation.2 | async-start | bytes 1048576 | tf_op jit(solution)/shard_map/all_to_all | solution.py:134
  103.1 21.2 %collective-permute-start.1 = (bf16[2048,128]{1,0:T(8,128)(2,1)}, bf16[2048,128]{1,0:T(8,128)(2,1)S(1)}, u32[]{:S(2)}, u32[]{:S(2)}) collective-permute-start(bf16[2048,128]{1,0:T(8,128)(2,1)} %collective-permute-done), channel_id=1, source_target_pairs={{0,64},{64,0},{128,192},{192,128},{256,320},{320,256},{384,448},{4... | collective-permute-start | bytes 1572872 | tf_op jit(solution)/shard_map/ppermute | solution.py:36
  115.6 18.7 %all-to-all-start.3 = ((f32[16,32,128]{2,1,0:T(8,128)}), f32[16,32,128]{2,1,0:T(8,128)S(1)}, u32[]{:S(2)}, u32[]{:S(2)}) async-start(f32[16,32,128]{2,1,0:T(8,128)} %broadcast_in_dim.66), calls=%async_computation.3 | async-start | bytes 524288 | tf_op jit(solution)/shard_map/all_to_all | solution.py:25
  124.9 9.4 %copy-start.3 = (bf16[32,512]{1,0:T(8,128)(2,1)S(1)}, bf16[32,512]{1,0:T(8,128)(2,1)}, u32[]{:S(2)}) copy-start(bf16[32,512]{1,0:T(8,128)(2,1)} %param.9) | copy-start | bytes 98308

commit v7 on v4

--- a/solution.py
+++ b/solution.py
@@ -78,17 +78,18 @@
         return lax.dynamic_slice_in_dim(value, (place ^ flip) * quarter, quarter, value.ndim - 1)
 
     reward = reward_bucket.astype(jnp.float32)
-    stats = jnp.concatenate([reward, reward * reward, response_len.astype(jnp.float32)])
-    stats = from_all(jnp.pad(stats, (0, LANES - 3)), REPLICA)
-    others = jnp.arange(replicas)
-    rewards = jnp.stack(
-        [jnp.sum(jnp.where(others == member ^ flip, stats[:, 0], 0.0)) for flip in range(GROUP)]
-    )
+    lane = jnp.arange(LANES)
+    stats = jnp.where(lane == 1, reward * reward, response_len.astype(jnp.float32))
+    stats = jnp.where(lane == 0, reward, jnp.where(lane < 3, stats, 0.0))
+    stats = from_all(stats, REPLICA)
+    chosen = member ^ jnp.arange(GROUP)[:, None] == jnp.arange(replicas)[None, :]
+    rewards = jnp.sum(jnp.where(chosen, stats[:, 0][None, :], 0.0), axis=1)
     sums = stats.sum(axis=0)
     high = jnp.floor(sums / DIGIT)
     low = sums - DIGIT * high
     extra = jnp.stack([jnp.pad(norm_gain, (0, LANES - rows_own)), high.astype(jnp.bfloat16), low.astype(jnp.bfloat16)])
-    filled = from_all(jnp.concatenate([quarter_of(kv_weight, 0), extra]), FSDP)
+    own = quarter_of(kv_weight, 0)
+    filled = from_all(jnp.concatenate([own, extra]), FSDP)
     weights = [filled[:, :rows_own].reshape(width, quarter)]
     extra = filled[:, rows_own:].astype(jnp.float32)
     gain_own = norm_gain.astype(jnp.float32)
@@ -107,11 +108,11 @@
     coarse = coarse.astype(jnp.bfloat16)
     position = jnp.arange(seq, dtype=jnp.int32)
     live = (position >= prompt_len[0]) & (position < prompt_len[0] + response_len[0])
-    masked = jnp.where(live[:, None], cotangent[0], jnp.zeros((), cotangent.dtype))
 
     def product(flip):
         def with_unit(rows):
-            part = quarter_of(masked, flip)
+            part = quarter_of(cotangent[0], flip)
+            part = jnp.where(live[:, None], part, jnp.zeros((), part.dtype))
             return jnp.einsum("td,tk->dk", rows, part, preferred_element_type=jnp.float32)
 
         return with_unit(coarse) + with_unit(fine)
@@ -125,9 +126,9 @@
     chip = chip.reshape(fsdp, rows_own, quarter)
     plane = lax.all_to_all(chip, FSDP, 0, 0, tiled=True)
     plane = plane.astype(jnp.float32).sum(axis=0)
-    every = from_all(plane, REPLICA)
-    every = every.reshape(replicas // GROUP, GROUP, rows_own, quarter).sum(axis=0)
-    total = jnp.concatenate([every[k] for k in range(GROUP)], axis=-1) * grad_scale
+    every = from_all((plane * grad_scale).astype(jnp.bfloat16), REPLICA)
+    every = every.astype(jnp.float32).reshape(replicas // GROUP, GROUP, rows_own, quarter).sum(axis=0)
+    total = jnp.concatenate([every[k] for k in range(GROUP)], axis=-1)
 
     grad_weight = total * (1.0 + gain_own)[:, None]
     grad_gain = jnp.sum(total * kv_weight.astype(jnp.float32), axis=1)

time: 143 us -> 140 us (0.979)
  other arithmetic: 7.73 us -> 3.53 us
    another operation x1 -> x0, other arithmetic: 2.63 us -> none  [shards(): jnp.stack([jnp.sum(jnp.where(others == member ^ flip, stats[:, 0], 0.0))...]
    all_to_all x3, waiting for transfers between devices: 37.3 us -> 39.4 us  [from_all(): return lax.all_to_all(copies, axes, 0, 0, tiled=True)]
    all_to_all x1, waiting for transfers between devices: 7.63 us -> 6 us  [shards(): plane = lax.all_to_all(chip, FSDP, 0, 0, tiled=True)]
  transfers between devices with their start and end apart: 10 -> 10, of which waited for: 4 -> 4; matrix products, arithmetic and copies ran while one was open for 14% -> 12% of each run, Pallas kernels for 1% -> 1%
where the time goes in v7:
time: 140 us; the launch traced here: 139 us
  starting transfers between devices  62.7 us (45%)
  waiting for transfers between devices  45.4 us (32%)
  matrix products  13.9 us (10%)
  local copies, waits for them, and re-layouts  6 us (4%)
  between operations  5.6 us (4%)
  other arithmetic  3.53 us (3%)
  Pallas kernels  1.9 us (1%)
    all_to_all x3, waiting for transfers between devices, from_all(): return lax.all_to_all(copies, axes, 0, 0, tiled=True)  39.4 us
    ppermute x6, starting transfers between devices, to_peer(): return lax.ppermute(value, REPLICA, [(i, i ^ flip) for i in range(count)])  32.5 us
    all_to_all x3, starting transfers between devices, from_all(): return lax.all_to_all(copies, axes, 0, 0, tiled=True)  24.1 us
    dot_general x8, matrix products, with_unit(): jnp.einsum('td,tk->dk', rows, part, preferred_element_type=jnp.float32)  8.41 us
    all_to_all x1, starting transfers between devices, shards(): plane = lax.all_to_all(chip, FSDP, 0, 0, tiled=True)  6.11 us
    all_to_all x1, waiting for transfers between devices, shards(): plane = lax.all_to_all(chip, FSDP, 0, 0, tiled=True)  6 us
    dot_general x4, matrix products, shards(): jnp.dot(normed, w, preferred_element_type=jnp.float32).astype(jnp.bfloat16)  5.44 us
  transfers between devices with their start and end apart: 10, of which 4 were waited for; matrix products, arithmetic and copies ran while one was open for 12% of the time, Pallas kernels for 1%

profile of v7, /device:TPU:1, one launch (start us, length us, event | category | flops | bytes accessed | tf_op | source)
XLA Modules:
  0.0 138.9 jit_solution(3271588780817792621)
XLA Ops:
  0.7 1.6 %fusion.6 = f32[256]{0:T(256)S(1)} fusion(bf16[1,256,2048]{2,1,0:T(8,128)(2,1)} %param.7), kind=kLoop, calls=%fused_computation.14 | loop fusion | flops 1572608 | bytes 1049600 | tf_op jit(solution)/shard_map/reduce_sum | solution.py:104
  3.6 1.5 %fusion.24 = f32[2048,128]{1,0:T(8,128)S(1)} fusion(bf16[1,256,512]{2,1,0:T(8,128)(2,1)} %param.8, s32[]{:T(128)S(6)} %select_n.191, pred[256]{0:T(512)(128)(4,1)S(1)} %compare_and_fusion, bf16[1,256,2048]{2,1,0:T(8,128)(2,1)S(1)} %copy-done, f32[256]{0:T(256)S(1)} %add_rsqrt_fusion), kind=kOutput, calls=%fused_computation.40 | convolution fusion | flops 136347648 | bytes 2163972 | tf_op jit(solution)/shard_map/td,tk->dk/dot_general | solution.py:116
  5.2 1.4 %fusion.3 = bf16[2048,128]{1,0:T(8,128)(2,1)} fusion(f32[2048,128]{1,0:T(8,128)S(1)} %fusion.24, bf16[1,256,512]{2,1,0:T(8,128)(2,1)S(1)} %copy-done.3, s32[]{:T(128)S(6)} %select_n.191, pred[256]{0:T(512)(128)(4,1)S(1)} %compare_and_fusion, bf16[1,256,2048]{2,1,0:T(8,128)(2,1)S(1)} %copy-done, f32[256]{0:T(256)S(1)} %add_rsqrt_fusion), kind=kOutput, calls=%fused_computation.11 | convolution fusion | flops 137396224 | bytes 2688516 | tf_op jit(solution)/shard_map/td,tk->dk/dot_general | solution.py:116
  6.6 16.0 %collective-permute-start.3 = (bf16[2048,128]{1,0:T(8,128)(2,1)}, bf16[2048,128]{1,0:T(8,128)(2,1)S(1)}, u32[]{:S(2)}, u32[]{:S(2)}) collective-permute-start(bf16[2048,128]{1,0:T(8,128)(2,1)} %fusion.3), channel_id=1, source_target_pairs={{0,64},{64,0},{128,192},{192,128},{256,320},{320,256},{384,448},{4... | collective-permute-start | bytes 1572872 | tf_op jit(solution)/shard_map/ppermute | solution.py:30
  23.3 1.5 %fusion.4 = bf16[2048,128]{1,0:T(8,128)(2,1)} fusion(f32[2048,128]{1,0:T(8,128)S(1)} %fusion.21, bf16[1,256,512]{2,1,0:T(8,128)(2,1)S(1)} %copy-done.3, s32[]{:T(128)S(6)} %select_n.194, pred[256]{0:T(512)(128)(4,1)S(1)} %compare_and_fusion, bf16[1,256,2048]{2,1,0:T(8,128)(2,1)S(1)} %copy-done, f32[256]{0:T(256)S(1)} %add_rsqrt_fusion), kind=kOutput, calls=%fused_computation.12 | convolution fusion | flops 137396224 | bytes 2688516 | tf_op jit(solution)/shard_map/td,tk->dk/dot_general | solution.py:116
  24.7 1.9 %collective-permute-start.4 = (bf16[2048,128]{1,0:T(8,128)(2,1)}, bf16[2048,128]{1,0:T(8,128)(2,1)S(1)}, u32[]{:S(2)}, u32[]{:S(2)}) collective-permute-start(bf16[2048,128]{1,0:T(8,128)(2,1)} %fusion.4), channel_id=1, source_target_pairs={{0,128},{64,192},{128,0},{192,64},{256,384},{320,448},{384,256},{4... | collective-permute-start | bytes 1572872 | tf_op jit(solution)/shard_map/ppermute | solution.py:30
  27.3 1.4 %fusion.5 = bf16[2048,128]{1,0:T(8,128)(2,1)} fusion(f32[2048,128]{1,0:T(8,128)S(1)} %fusion.18, bf16[1,256,512]{2,1,0:T(8,128)(2,1)S(1)} %copy-done.3, s32[]{:T(128)S(6)} %select_n.197, pred[256]{0:T(512)(128)(4,1)S(1)} %compare_and_fusion, bf16[1,256,2048]{2,1,0:T(8,128)(2,1)S(1)} %copy-done, f32[256]{0:T(256)S(1)} %add_rsqrt_fusion), kind=kOutput, calls=%fused_computation.13 | convolution fusion | flops 137396224 | bytes 2688516 | tf_op jit(solution)/shard_map/td,tk->dk/dot_general | solution.py:116
  28.8 3.5 %collective-permute-start.5 = (bf16[2048,128]{1,0:T(8,128)(2,1)}, bf16[2048,128]{1,0:T(8,128)(2,1)S(1)}, u32[]{:S(2)}, u32[]{:S(2)}) collective-permute-start(bf16[2048,128]{1,0:T(8,128)(2,1)} %fusion.5), channel_id=1, source_target_pairs={{0,192},{64,128},{128,64},{192,0},{256,448},{320,384},{384,320},{4... | collective-permute-start | bytes 1572872 | tf_op jit(solution)/shard_map/ppermute | solution.py:30
  33.6 4.3 %all-to-all-start = ((f32[16,1,128]{2,1,0:T(1,128)}), f32[16,1,128]{2,1,0:T(1,128)S(1)}, u32[]{:S(2)}, u32[]{:S(2)}) async-start(f32[16,1,128]{2,1,0:T(1,128)} %broadcast_in_dim.129), calls=%async_computation | async-start | bytes 16384 | tf_op jit(solution)/shard_map/all_to_all | solution.py:25
  38.6 15.5 %all-to-all-done = f32[16,1,128]{2,1,0:T(1,128)S(1)} async-done(((f32[16,1,128]{2,1,0:T(1,128)}), f32[16,1,128]{2,1,0:T(1,128)S(1)}, u32[]{:S(2)}, u32[]{:S(2)}) %all-to-all-start) | async-done | bytes 8224 | tf_op jit(solution)/shard_map/all_to_all | solution.py:25
  55.1 13.2 %all-to-all-start.1 = ((bf16[64,35,128]{2,1,0:T(8,128)(2,1)}), bf16[64,35,128]{2,1,0:T(8,128)(2,1)S(1)}, u32[]{:S(2)}, u32[]{:S(2)}) async-start(bf16[64,35,128]{2,1,0:T(8,128)(2,1)} %broadcast_in_dim.130), calls=%async_computation.1 | async-start | bytes 1310720 | tf_op jit(solution)/shard_map/all_to_all | solution.py:25
  70.5 16.4 %all-to-all-done.1.filled_ref = bf16[64,35,128]{2,1,0:T(8,128)(2,1)S(1)} async-done(((bf16[64,35,128]{2,1,0:T(8,128)(2,1)}), bf16[64,35,128]{2,1,0:T(8,128)(2,1)S(1)}, u32[]{:S(2)}, u32[]{:S(2)}) %all-to-all-start.1) | async-done | bytes 573472 | tf_op jit(solution)/shard_map/all_to_all | solution.py:25
  87.7 5.4 %collective-permute-start.2 = (bf16[2048,128]{1,0:T(8,128)(2,1)}, bf16[2048,128]{1,0:T(8,128)(2,1)}, u32[]{:S(2)}, u32[]{:S(2)}) collective-permute-start(bf16[2048,128]{1,0:T(8,128)(2,1)} %bitcast.6), channel_id=1, source_target_pairs={{0,64},{64,0},{128,192},{192,128},{256,320},{320,256},{384,448},{4... | collective-permute-start | bytes 1572872 | tf_op jit(solution)/shard_map/ppermute | solution.py:30
  93.2 3.1 %collective-permute-start = (bf16[2048,128]{1,0:T(8,128)(2,1)}, bf16[2048,128]{1,0:T(8,128)(2,1)}, u32[]{:S(2)}, u32[]{:S(2)}) collective-permute-start(bf16[2048,128]{1,0:T(8,128)(2,1)} %bitcast.6), channel_id=1, source_target_pairs={{0,128},{64,192},{128,0},{192,64},{256,384},{320,448},{384,256},{4... | collective-permute-start | bytes 1572872 | tf_op jit(solution)/shard_map/ppermute | solution.py:30
  96.3 1.9 %combine.1 = bf16[2048,128]{1,0:T(8,128)(2,1)} custom-call(f32[4]{0:T(128)S(1)} %select_reduce_fusion.rewards_ref, bf16[64,35,128]{2,1,0:T(8,128)(2,1)S(1)} %all-to-all-done.1.filled_ref, f32[2048,128]{1,0:T(8,128)S(1)} %convolution_add_fusion.3.kept_ref, bf16[2048,128]{1,0:T(8,128)(2,1)S(1)} %collective-permute-done.3.refs_0_, ...), custom_call_target="tpu_custom_call" | custom-call | flops 2097152 | bytes 3145728 | tf_op jit(solution)/shard_map/combine/pallas_call | solution.py:56
  98.2 6.1 %all-to-all-start.2 = ((bf16[64,32,128]{2,1,0:T(8,128)(2,1)}), bf16[64,32,128]{2,1,0:T(8,128)(2,1)S(1)}, u32[]{:S(2)}, u32[]{:S(2)}) async-start(bf16[64,32,128]{2,1,0:T(8,128)(2,1)} %bitcast.18), calls=%async_computation.2 | async-start | bytes 1048576 | tf_op jit(solution)/shard_map/all_to_all | solution.py:127
  107.9 1.6 %convolution_convert_fusion = bf16[256,128]{0,1:T(8,128)(2,1)S(1)} fusion(bf16[2048,128]{1,0:T(8,128)(2,1)} %bitcast.6, bf16[1,256,2048]{2,1,0:T(8,128)(2,1)S(1)} %copy-done.2, f32[2048]{0:T(1024)S(1)} %add.88, f32[256]{0:T(256)S(1)} %add_rsqrt_fusion), kind=kOutput, calls=%fused_computation.19 | convolution fusion | flops 136347648 | bytes 1647616 | tf_op jit(solution)/shard_map/dot_general | solution.py:141
  109.5 2.5 %collective-permute-start.1 = (bf16[2048,128]{1,0:T(8,128)(2,1)}, bf16[2048,128]{1,0:T(8,128)(2,1)S(1)}, u32[]{:S(2)}, u32[]{:S(2)}) collective-permute-start(bf16[2048,128]{1,0:T(8,128)(2,1)} %collective-permute-done), channel_id=1, source_target_pairs={{0,64},{64,0},{128,192},{192,128},{256,320},{320,256},{384,448},{4... | collective-permute-start | bytes 1572872 | tf_op jit(solution)/shard_map/ppermute | solution.py:30
  112.0 1.6 %convolution_convert_fusion.2 = bf16[256,128]{0,1:T(8,128)(2,1)S(1)} fusion(bf16[2048,128]{1,0:T(8,128)(2,1)} %collective-permute-done, bf16[1,256,2048]{2,1,0:T(8,128)(2,1)S(1)} %copy-done.2, f32[2048]{0:T(1024)S(1)} %add.88, f32[256]{0:T(256)S(1)} %add_rsqrt_fusion), kind=kOutput, calls=%fused_computation.21 | convolution fusion | flops 136347648 | bytes 1647616 | tf_op jit(solution)/shard_map/dot_general | solution.py:141
  113.7 1.6 %convolution_convert_fusion.1 = bf16[256,128]{0,1:T(8,128)(2,1)S(1)} fusion(bf16[2048,128]{1,0:T(8,128)(2,1)} %collective-permute-done.2, bf16[1,256,2048]{2,1,0:T(8,128)(2,1)S(1)} %copy-done.2, f32[2048]{0:T(1024)S(1)} %add.88, f32[256]{0:T(256)S(1)} %add_rsqrt_fusion), kind=kOutput, calls=%fused_computation.20 | convolution fusion | flops 136347648 | bytes 1647616 | tf_op jit(solution)/shard_map/dot_general | solution.py:141
  115.3 6.0 %all-to-all-done.2 = bf16[64,32,128]{2,1,0:T(8,128)(2,1)S(1)} async-done(((bf16[64,32,128]{2,1,0:T(8,128)(2,1)}), bf16[64,32,128]{2,1,0:T(8,128)(2,1)S(1)}, u32[]{:S(2)}, u32[]{:S(2)}) %all-to-all-start.2) | async-done | bytes 524320 | tf_op jit(solution)/shard_map/all_to_all | solution.py:127
  122.1 6.6 %all-to-all-start.3 = ((bf16[16,32,128]{2,1,0:T(8,128)(2,1)}), bf16[16,32,128]{2,1,0:T(8,128)(2,1)S(1)}, u32[]{:S(2)}, u32[]{:S(2)}) async-start(bf16[16,32,128]{2,1,0:T(8,128)(2,1)} %broadcast_in_dim.137), calls=%async_computation.3 | async-start | bytes 262144 | tf_op jit(solution)/shard_map/all_to_all | solution.py:25
  130.2 7.4 %all-to-all-done.3 = bf16[16,32,128]{2,1,0:T(8,128)(2,1)S(1)} async-done(((bf16[16,32,128]{2,1,0:T(8,128)(2,1)}), bf16[16,32,128]{2,1,0:T(8,128)(2,1)S(1)}, u32[]{:S(2)}, u32[]{:S(2)}) %all-to-all-start.3) | async-done | bytes 131104 | tf_op jit(solution)/shard_map/all_to_all | solution.py:25
  137.6 1.3 multiply_reduce_fusion
  (52 shorter events, 9.7 us)
Async XLA Ops:
  0.6 3.0 %copy-start = (bf16[1,256,2048]{2,1,0:T(8,128)(2,1)S(1)}, bf16[1,256,2048]{2,1,0:T(8,128)(2,1)}, u32[]{:S(2)}) copy-start(bf16[1,256,2048]{2,1,0:T(8,128)(2,1)} %param.7) | copy-start | bytes 3145732
  3.6 1.6 %copy-start.3 = (bf16[1,256,512]{2,1,0:T(8,128)(2,1)S(1)}, bf16[1,256,512]{2,1,0:T(8,128)(2,1)}, u32[]{:S(2)}) copy-start(bf16[1,256,512]{2,1,0:T(8,128)(2,1)} %param.8) | copy-start | bytes 786436
  6.6 89.7 %collective-permute-start.3 = (bf16[2048,128]{1,0:T(8,128)(2,1)}, bf16[2048,128]{1,0:T(8,128)(2,1)S(1)}, u32[]{:S(2)}, u32[]{:S(2)}) collective-permute-start(bf16[2048,128]{1,0:T(8,128)(2,1)} %fusion.3), channel_id=1, source_target_pairs={{0,64},{64,0},{128,192},{192,128},{256,320},{320,256},{384,448},{4... | collective-permute-start | bytes 1572872 | tf_op jit(solution)/shard_map/ppermute | solution.py:30
  24.7 71.6 %collective-permute-start.4 = (bf16[2048,128]{1,0:T(8,128)(2,1)}, bf16[2048,128]{1,0:T(8,128)(2,1)S(1)}, u32[]{:S(2)}, u32[]{:S(2)}) collective-permute-start(bf16[2048,128]{1,0:T(8,128)(2,1)} %fusion.4), channel_id=1, source_target_pairs={{0,128},{64,192},{128,0},{192,64},{256,384},{320,448},{384,256},{4... | collective-permute-start | bytes 1572872 | tf_op jit(solution)/shard_map/ppermute | solution.py:30
  27.3 11.3 %copy-start.5 = (bf16[32]{0:T(256)(128)(2,1)S(1)}, bf16[32]{0:T(256)(128)(2,1)}, u32[]{:S(2)}) copy-start(bf16[32]{0:T(256)(128)(2,1)} %param.10) | copy-start | bytes 196
  28.8 67.6 %collective-permute-start.5 = (bf16[2048,128]{1,0:T(8,128)(2,1)}, bf16[2048,128]{1,0:T(8,128)(2,1)S(1)}, u32[]{:S(2)}, u32[]{:S(2)}) collective-permute-start(bf16[2048,128]{1,0:T(8,128)(2,1)} %fusion.5), channel_id=1, source_target_pairs={{0,192},{64,128},{128,64},{192,0},{256,448},{320,384},{384,320},{4... | collective-permute-start | bytes 1572872 | tf_op jit(solution)/shard_map/ppermute | solution.py:30
  33.6 20.5 %all-to-all-start = ((f32[16,1,128]{2,1,0:T(1,128)}), f32[16,1,128]{2,1,0:T(1,128)S(1)}, u32[]{:S(2)}, u32[]{:S(2)}) async-start(f32[16,1,128]{2,1,0:T(1,128)} %broadcast_in_dim.129), calls=%async_computation | async-start | bytes 16384 | tf_op jit(solution)/shard_map/all_to_all | solution.py:25
  55.1 31.8 %all-to-all-start.1 = ((bf16[64,35,128]{2,1,0:T(8,128)(2,1)}), bf16[64,35,128]{2,1,0:T(8,128)(2,1)S(1)}, u32[]{:S(2)}, u32[]{:S(2)}) async-start(bf16[64,35,128]{2,1,0:T(8,128)(2,1)} %broadcast_in_dim.130), calls=%async_computation.1 | async-start | bytes 1310720 | tf_op jit(solution)/shard_map/all_to_all | solution.py:25
  68.3 1.2 copy-start.1
  69.5 0.7 copy-start.6
  87.7 25.9 %collective-permute-start.2 = (bf16[2048,128]{1,0:T(8,128)(2,1)}, bf16[2048,128]{1,0:T(8,128)(2,1)}, u32[]{:S(2)}, u32[]{:S(2)}) collective-permute-start(bf16[2048,128]{1,0:T(8,128)(2,1)} %bitcast.6), channel_id=1, source_target_pairs={{0,64},{64,0},{128,192},{192,128},{256,320},{320,256},{384,448},{4... | collective-permute-start | bytes 1572872 | tf_op jit(solution)/shard_map/ppermute | solution.py:30
  93.2 16.3 %collective-permute-start = (bf16[2048,128]{1,0:T(8,128)(2,1)}, bf16[2048,128]{1,0:T(8,128)(2,1)}, u32[]{:S(2)}, u32[]{:S(2)}) collective-permute-start(bf16[2048,128]{1,0:T(8,128)(2,1)} %bitcast.6), channel_id=1, source_target_pairs={{0,128},{64,192},{128,0},{192,64},{256,384},{320,448},{384,256},{4... | collective-permute-start | bytes 1572872 | tf_op jit(solution)/shard_map/ppermute | solution.py:30
  98.2 9.7 %copy-start.2 = (bf16[1,256,2048]{2,1,0:T(8,128)(2,1)S(1)}, bf16[1,256,2048]{2,1,0:T(8,128)(2,1)}, u32[]{:S(2)}) copy-start(bf16[1,256,2048]{2,1,0:T(8,128)(2,1)} %param.7) | copy-start | bytes 3145732
  98.2 23.1 %all-to-all-start.2 = ((bf16[64,32,128]{2,1,0:T(8,128)(2,1)}), bf16[64,32,128]{2,1,0:T(8,128)(2,1)S(1)}, u32[]{:S(2)}, u32[]{:S(2)}) async-start(bf16[64,32,128]{2,1,0:T(8,128)(2,1)} %bitcast.18), calls=%async_computation.2 | async-start | bytes 1048576 | tf_op jit(solution)/shard_map/all_to_all | solution.py:127
  109.5 19.1 %collective-permute-start.1 = (bf16[2048,128]{1,0:T(8,128)(2,1)}, bf16[2048,128]{1,0:T(8,128)(2,1)S(1)}, u32[]{:S(2)}, u32[]{:S(2)}) collective-permute-start(bf16[2048,128]{1,0:T(8,128)(2,1)} %collective-permute-done), channel_id=1, source_target_pairs={{0,64},{64,0},{128,192},{192,128},{256,320},{320,256},{384,448},{4... | collective-permute-start | bytes 1572872 | tf_op jit(solution)/shard_map/ppermute | solution.py:30
  122.1 15.5 %all-to-all-start.3 = ((bf16[16,32,128]{2,1,0:T(8,128)(2,1)}), bf16[16,32,128]{2,1,0:T(8,128)(2,1)S(1)}, u32[]{:S(2)}, u32[]{:S(2)}) async-start(bf16[16,32,128]{2,1,0:T(8,128)(2,1)} %broadcast_in_dim.137), calls=%async_computation.3 | async-start | bytes 262144 | tf_op jit(solution)/shard_map/all_to_all | solution.py:25
  129.3 8.3 %copy-start.4 = (bf16[32,512]{1,0:T(8,128)(2,1)S(1)}, bf16[32,512]{1,0:T(8,128)(2,1)}, u32[]{:S(2)}) copy-start(bf16[32,512]{1,0:T(8,128)(2,1)} %param.9) | copy-start | bytes 98308
